TPU v7x, 32 devices: a whole 2x2x4 slice. The times are simulated.
32 devices in a mesh: rep: 1, r: 8 (over y, z), s: 4 (over x, core).
Axes of the slice: x: 2, y: 2, z: 4, core: 2. Of those that a mesh axis runs over, the one named last changes fastest.
Arguments:
- x: bfloat16 [32, 4096, 512], P(('rep', 'r', 's'))
- dy: bfloat16 [32, 4096, 512], P(('rep', 'r', 's'))
- w_gate: bfloat16 [2, 512, 4096], P(None, 's')
- w_up: bfloat16 [2, 512, 4096], P(None, 's')
- w_down: bfloat16 [2, 4096, 512], P(None, 's')
- m_w_gate: float32 [2, 512, 4096], P(None, 's')
- m_w_up: float32 [2, 512, 4096], P(None, 's')
- m_w_down: float32 [2, 4096, 512], P(None, 's')
- v_w_gate: float32 [2, 512, 4096], P(None, 's')
- v_w_up: float32 [2, 512, 4096], P(None, 's')
- v_w_down: float32 [2, 4096, 512], P(None, 's')
Outputs:
- output 1: bfloat16 [2, 512, 4096], P('rep', 's')
- output 2: bfloat16 [2, 512, 4096], P('rep', 's')
- output 3: bfloat16 [2, 4096, 512], P('rep', 's')
- output 4: float32 [2, 512, 4096], P('rep', 's')
- output 5: float32 [2, 512, 4096], P('rep', 's')
- output 6: float32 [2, 4096, 512], P('rep', 's')
- output 7: float32 [2, 512, 4096], P('rep', 's')
- output 8: float32 [2, 512, 4096], P('rep', 's')
- output 9: float32 [2, 4096, 512], P('rep', 's')
All inputs are finite; a program needn't handle non-finite values.
Results may differ from a plain program's by a relative error of at most 0.022.
Values are sent between devices in bfloat16 or wider.
A program may use at most 2 GiB of HBM per device.

v0:
```python
import jax
import jax.numpy as jnp
from jax import lax
from jax.sharding import PartitionSpec as P

NAMES = ("w_gate", "w_up", "w_down")


def matmul(a, w):
    return jnp.dot(a, w, preferred_element_type=jnp.float32).astype(jnp.bfloat16)


def normed(h):
    wide = h.astype(jnp.float32)
    scale = lax.rsqrt(jnp.mean(wide**2, -1, keepdims=True) + 1e-6)
    return (wide * scale).astype(jnp.bfloat16)


def layer(h, w):
    a = normed(h)
    gate = jnp.dot(a, w["w_gate"], preferred_element_type=jnp.float32)
    up = jnp.dot(a, w["w_up"], preferred_element_type=jnp.float32)
    return h + matmul((jax.nn.silu(gate) * up).astype(jnp.bfloat16), w["w_down"])


def adamw(w, m, v, g):
    m = 0.9 * m + 0.1 * g
    v = 0.95 * v + 0.05 * g * g
    step = m * lax.rsqrt(v + 1e-8) + 0.1 * w
    return (w - 0.02 * step).astype(jnp.bfloat16), m, v


def clipped(gradients, sum_of_squares, count):
    factor = jnp.minimum(1.0, 0.5 * lax.rsqrt(sum_of_squares / count + 1e-30))
    return [g * factor for g in gradients]


def solution(mesh):
    def fetched(weights, number):
        return {name: lax.all_gather(w[number], "s", axis=0, tiled=True) for name, w in zip(NAMES, weights, strict=True)}

    def summed(term):
        return lax.psum(lax.psum_scatter(term, "s", scatter_dimension=0, tiled=True), "r")

    def step(x, dy, *arrays):
        weights, m, v = (arrays[i : i + 3] for i in (0, 3, 6))
        layers = weights[0].shape[0]
        h, kept = x[0], []
        for number in range(layers):
            kept.append(h)
            h = layer(h, fetched(weights, number))
        by_h, mine = dy[0], [None] * layers
        for number in reversed(range(layers)):
            _, back = jax.vjp(lambda w, h: layer(h, w), fetched(weights, number), kept[number])
            by_w, by_h = back(by_h)
            mine[number] = [summed(by_w[name]) for name in NAMES]
        gradients = [jnp.stack([mine[number][i] for number in range(layers)]).astype(jnp.float32) for i in range(3)]
        squares = lax.psum(sum(jnp.sum(g * g) for g in gradients), "s")
        gradients = clipped(gradients, squares, lax.psum(1, "s") * sum(g.size for g in gradients))
        new = [adamw(w.astype(jnp.float32), m, v, g) for w, m, v, g in zip(weights, m, v, gradients, strict=True)]
        return tuple(one[which] for which in range(3) for one in new)

    states, cut = P(("rep", "r", "s"), None, None), P(None, "s", None)
    return jax.shard_map(
        step,
        mesh=mesh,
        in_specs=(states, states) + (cut,) * 9,
        out_specs=(P("rep", "s", None),) * 9,
        check_vma=False,
    )
```

profile of v0, /device:TPU:0, one launch (start us, length us, event | category | flops | bytes accessed | tf_op | source)
XLA Modules:
  0.0 972.5 jit_solution(17572759975430168272)
XLA Ops:
  26.4 6.3 copy.21
  32.7 14.8 %all-gather.13.cloned.1.call-done = bf16[1,512,4096]{2,1,0:T(8,128)(2,1)} async-done(((bf16[1,128,4096]{2,1,0:T(8,128)(2,1)}), bf16[1,512,4096]{2,1,0:T(8,128)(2,1)}) %all-gather.13.cloned.1.call-update) | async-done | bytes 4194320 | tf_op jit(solution)/shard_map/all_gather | solution.py:40
  47.5 30.2 %fusion.67 = f32[4096,4096]{1,0:T(8,128)} fusion(bf16[1,512,4096]{2,1,0:T(8,128)(2,1)} %all-gather.13.cloned.1.call-done, bf16[1,4096,512]{1,2,0:T(8,128)(2,1)} %copy.20, f32[4096]{0:T(1024)S(1)} %add_rsqrt_fusion), kind=kOutput, calls=%fused_computation.101 | convolution fusion | flops 17186160640 | bytes 75513856 | tf_op jit(solution)/shard_map/dot_general | solution.py:21
  84.0 59.8 %multiply_convert_fusion.1 = (bf16[4096,4096]{1,0:T(8,128)(2,1)}, f32[4096,4096]{1,0:T(8,128)}) fusion(f32[4096,4096]{1,0:T(8,128)} %fusion.67, bf16[1,512,4096]{2,1,0:T(8,128)(2,1)} %all-gather.15.cloned.1.call-done, bf16[1,4096,512]{1,2,0:T(8,128)(2,1)} %copy.20, f32[4096]{0:T(1024)S(1)} %add_rsqrt_fusion), kind=kOutput, calls=%fused_computation.17 | convolution fusion | flops 17286823936 | bytes 176177152 | tf_op jit(solution)/shard_map/dot_general | solution.py:22
  143.8 24.7 %fusion.20 = (f32[4096]{0:T(1024)S(1)}, bf16[4096,512]{0,1:T(8,128)(2,1)}) fusion(bf16[4096,4096]{1,0:T(8,128)(2,1)} %get-tuple-element.30, bf16[1,4096,512]{2,1,0:T(8,128)(2,1)} %all-gather.17.cloned.1.call-done, bf16[1,4096,512]{1,2,0:T(8,128)(2,1)} %copy.20), kind=kOutput, calls=%fused_computation.37 | convolution fusion | flops 17190350848 | bytes 46153728 | tf_op jit(solution)/shard_map/dot_general | solution.py:10
  168.5 24.8 %convolution_convert_fusion.1 = bf16[4096,4096]{1,0:T(8,128)(2,1)} fusion(bf16[1,4096,512]{2,1,0:T(8,128)(2,1)} %param.12, bf16[1,4096,512]{2,1,0:T(8,128)(2,1)} %all-gather.21.cloned.1.call-done), kind=kOutput, calls=%fused_computation.25 | convolution fusion | flops 17196646400 | bytes 41943040 | tf_op jit(solution)/shard_map/transpose(jvp())/dot_general | solution.py:10
  193.4 30.4 %fusion.56 = f32[4096,4096]{1,0:T(8,128)} fusion(bf16[1,512,4096]{2,1,0:T(8,128)(2,1)} %all-gather.23.cloned.1.call-done, bf16[4096,512]{0,1:T(8,128)(2,1)} %get-tuple-element.33, f32[4096]{0:T(1024)S(1)} %fusion.77), kind=kOutput, calls=%fused_computation.90 | convolution fusion | flops 17186160640 | bytes 75513856 | tf_op jit(solution)/shard_map/jvp()/dot_general | solution.py:22
  229.3 79.0 %fusion.2 = (bf16[4096,4096]{1,0:T(8,128)(2,1)}, f32[4096,4096]{1,0:T(8,128)}) fusion(f32[4096,4096]{1,0:T(8,128)} %fusion.56, bf16[4096,4096]{1,0:T(8,128)(2,1)} %convolution_convert_fusion.1, bf16[1,512,4096]{2,1,0:T(8,128)(2,1)} %all-gather.19.cloned.1.call-done, bf16[4096,512]{0,1:T(8,128)(2,1)} %get-tuple-element.33, f32[4096]{0:T(1024)S(1)} %fusion.77), kind=kOutput, calls=%fused_computation.8 | convolution fusion | flops 17387487232 | bytes 209731584 | tf_op jit(solution)/shard_map/jvp()/dot_general | solution.py:21
  308.3 39.1 %fusion.25 = bf16[4096,512]{0,1:T(8,128)(2,1)} fusion(bf16[4096,4096]{1,0:T(8,128)(2,1)} %convolution_convert_fusion.1, bf16[1,512,4096]{2,1,0:T(8,128)(2,1)} %all-gather.23.cloned.1.call-done, f32[4096,4096]{1,0:T(8,128)} %get-tuple-element.35), kind=kOutput, calls=%fused_computation.48 | convolution fusion | flops 17282629632 | bytes 109051904 | tf_op jit(solution)/shard_map/transpose(jvp())/dot_general | solution.py:22
  347.4 33.1 %fusion.22 = (f32[4096]{0:T(1024)S(1)}, bf16[4096,512]{0,1:T(8,128)(2,1)}) fusion(bf16[4096,512]{0,1:T(8,128)(2,1)} %get-tuple-element.33, bf16[4096,512]{0,1:T(8,128)(2,1)} %fusion.25, bf16[4096,4096]{1,0:T(8,128)(2,1)} %get-tuple-element.34, bf16[1,512,4096]{2,1,0:T(8,128)(2,1)} %all-gather.19.cloned.1.call-done), kind=kOutput, calls=%fused_computation.39 | convolution fusion | flops 17190350848 | bytes 50348032 | tf_op jit(solution)/shard_map/transpose(jvp())/dot_general | solution.py:21
  380.6 6.7 fusion.53
  389.3 24.0 %convolution_convert_fusion.2 = bf16[4096,512]{1,0:T(8,128)(2,1)} fusion(bf16[4096,4096]{1,0:T(8,128)(2,1)} %get-tuple-element.30, bf16[4096,512]{0,1:T(8,128)(2,1)S(1)} %fusion.53), kind=kOutput, calls=%fused_computation.45 | convolution fusion | flops 17181966336 | bytes 41943040 | tf_op jit(solution)/shard_map/transpose(jvp())/dot_general | solution.py:10
  413.4 45.4 %fusion.23 = bf16[4096,512]{1,0:T(8,128)(2,1)} fusion(f32[4096,4096]{1,0:T(8,128)} %fusion.56, bf16[1,4096,512]{2,1,0:T(8,128)(2,1)} %param.12, f32[4096,4096]{1,0:T(8,128)} %get-tuple-element.35), kind=kOutput, calls=%fused_computation.43 | convolution fusion | flops 17282629632 | bytes 142606336 | tf_op jit(solution)/shard_map/transpose(jvp())/dot_general | solution.py:10
  458.9 24.5 %convolution_convert_fusion = bf16[4096,4096]{1,0:T(8,128)(2,1)} fusion(bf16[4096,512]{0,1:T(8,128)(2,1)} %copy-done.9, bf16[1,4096,512]{2,1,0:T(8,128)(2,1)} %all-gather.17.cloned.1.call-done), kind=kOutput, calls=%fused_computation.24 | convolution fusion | flops 17196646400 | bytes 41943040 | tf_op jit(solution)/shard_map/transpose(jvp())/dot_general | solution.py:10
  483.4 37.7 %fusion.29 = bf16[512,4096]{1,0:T(8,128)(2,1)} fusion(bf16[4096,4096]{1,0:T(8,128)(2,1)} %convolution_convert_fusion, f32[4096,4096]{1,0:T(8,128)} %fusion.67, bf16[1,4096,512]{1,2,0:T(8,128)(2,1)S(1)} %copy-done, f32[4096]{0:T(1024)S(1)} %copy-done.17), kind=kOutput, calls=%fused_computation.51 | convolution fusion | flops 17288921088 | bytes 109068288 | tf_op jit(solution)/shard_map/transpose(jvp())/dot_general | solution.py:22
  521.8 39.2 %fusion.24 = bf16[512,4096]{1,0:T(8,128)(2,1)} fusion(bf16[4096,4096]{1,0:T(8,128)(2,1)} %convolution_convert_fusion.1, bf16[4096,512]{0,1:T(8,128)(2,1)} %get-tuple-element.33, f32[4096]{0:T(1024)S(1)} %copy-done.14, f32[4096,4096]{1,0:T(8,128)} %get-tuple-element.35), kind=kOutput, calls=%fused_computation.44 | convolution fusion | flops 17288921088 | bytes 109068288 | tf_op jit(solution)/shard_map/transpose(jvp())/dot_general | solution.py:22
  561.1 59.0 %fusion.26 = bf16[512,4096]{1,0:T(8,128)(2,1)} fusion(f32[4096,4096]{1,0:T(8,128)} %fusion.67, f32[4096,4096]{1,0:T(8,128)} %get-tuple-element.31, bf16[4096,4096]{1,0:T(8,128)(2,1)} %convolution_convert_fusion, bf16[1,4096,512]{1,2,0:T(8,128)(2,1)} %copy.20, f32[4096]{0:T(1024)S(1)} %copy-done.17), kind=kOutput, calls=%fused_computation.50 | convolution fusion | flops 17372807168 | bytes 176177152 | tf_op jit(solution)/shard_map/transpose(jvp())/dot_general | solution.py:21
  620.9 23.6 %convolution_convert_fusion.5 = bf16[512,4096]{1,0:T(8,128)(2,1)} fusion(bf16[4096,4096]{1,0:T(8,128)(2,1)} %get-tuple-element.34, bf16[4096,512]{0,1:T(8,128)(2,1)} %get-tuple-element.33, f32[4096]{0:T(1024)S(1)} %copy-done.15), kind=kOutput, calls=%fused_computation.49 | convolution fusion | flops 17186160640 | bytes 41959424 | tf_op jit(solution)/shard_map/transpose(jvp())/dot_general | solution.py:21
  644.6 19.5 %reduce-scatter.7.cloned.1.call-done = bf16[128,4096]{1,0:T(8,128)(2,1)} async-done(((bf16[512,4096]{1,0:T(8,128)(2,1)}), bf16[128,4096]{1,0:T(8,128)(2,1)}) %reduce-scatter.7.cloned.1.call-update) | async-done | bytes 1048592 | tf_op jit(solution)/shard_map/reduce_scatter | solution.py:43
  664.2 46.8 %reduce-scatter.9.cloned.1.call-done = bf16[128,4096]{1,0:T(8,128)(2,1)} async-done(((bf16[512,4096]{1,0:T(8,128)(2,1)}), bf16[128,4096]{1,0:T(8,128)(2,1)}) %reduce-scatter.9.cloned.1.call-update) | async-done | bytes 1048592 | tf_op jit(solution)/shard_map/reduce_scatter | solution.py:43
  711.0 215.3 %all-reduce.3.cloned.1.call-done = (bf16[1,128,4096]{2,1,0:T(8,128)(2,1)}, bf16[1,128,4096]{2,1,0:T(8,128)(2,1)}, bf16[1,128,4096]{2,1,0:T(8,128)(2,1)}, bf16[1,...) async-done(((bf16[1,128,4096]{2,1,0:T(8,128)(2,1)}, bf16[1,128,4096]{2,1,0:T(8,128)(2,1)}, bf16[1,128,4096]{2,1,0:T(8,128)(2,1)}, ...) | async-done | bytes 6291472 | tf_op jit(solution)/shard_map/psum | solution.py:43
  936.5 6.6 psum.55
  943.8 8.4 fusion.49
  952.2 13.2 %fusion.40 = (bf16[2,128,4096]{2,1,0:T(8,128)(2,1)}, f32[2,128,4096]{2,1,0:T(8,128)}, f32[2,128,4096]{2,1,0:T(8,128)}, bf16[2,128,4096]{2,1,0:T(8,128)(2,1)}, f3...) fusion(bf16[2,128,4096]{2,1,0:T(8,128)(2,1)S(1)} %copy-done.3, f32[]{:T(128)S(6)} %min_shard_map.3, ...), kind=kLoop, calls=%fused_computation.74 | loop fusion | flops 41943040 | bytes 46137348 | tf_op jit(solution)/shard_map/convert_element_type | solution.py:30
  (82 shorter events, 43.1 us)
Async XLA Ops:
  7.2 40.3 %all-gather.13.cloned.1.call-start = ((), (), s32[]{:S(2)}) async-start(), calls=%async_computation.12 | async-start | bytes 5242880 | tf_op jit(solution)/shard_map/all_gather | solution.py:40
  10.3 73.6 %all-gather.15.cloned.1.call-start = ((), (), s32[]{:S(2)}) async-start(), calls=%async_computation.13 | async-start | bytes 5242880 | tf_op jit(solution)/shard_map/all_gather | solution.py:40
  13.6 130.2 %all-gather.17.cloned.1.call-start = ((), (), s32[]{:S(2)}) async-start(), calls=%async_computation.14 | async-start | bytes 5242880 | tf_op jit(solution)/shard_map/all_gather | solution.py:40
  15.1 153.4 %all-gather.21.cloned.1.call-start = ((), (), s32[]{:S(2)}) async-start(), calls=%async_computation.16 | async-start | bytes 5242880 | tf_op jit(solution)/shard_map/all_gather | solution.py:40
  15.7 177.6 %all-gather.23.cloned.1.call-start = ((), (), s32[]{:S(2)}) async-start(), calls=%async_computation.17 | async-start | bytes 5242880 | tf_op jit(solution)/shard_map/all_gather | solution.py:40
  16.3 213.0 %all-gather.19.cloned.1.call-start = ((), (), s32[]{:S(2)}) async-start(), calls=%async_computation.15 | async-start | bytes 5242880 | tf_op jit(solution)/shard_map/all_gather | solution.py:40
  16.9 627.7 %reduce-scatter.15.cloned.1.call-start = ((), (), s32[]{:S(2)}) async-start(), calls=%async_computation.10 | async-start | bytes 5242880 | tf_op jit(solution)/shard_map/reduce_scatter | solution.py:43
  26.4 57.6 %copy-start.16 = (f32[4096]{0:T(1024)}, f32[4096]{0:T(1024)S(1)}, u32[]{:S(2)}) copy-start(f32[4096]{0:T(1024)S(1)} %add_rsqrt_fusion) | copy-start | bytes 49156
  168.5 24.9 %copy-start.10 = (f32[4096]{0:T(1024)}, f32[4096]{0:T(1024)S(1)}, u32[]{:S(2)}) copy-start(f32[4096]{0:T(1024)S(1)} %get-tuple-element.32) | copy-start | bytes 49156
  168.5 60.8 %copy-start.12 = (f32[4096]{0:T(1024)}, f32[4096]{0:T(1024)S(1)}, u32[]{:S(2)}) copy-start(f32[4096]{0:T(1024)S(1)} %fusion.77) | copy-start | bytes 49156
  347.4 33.1 %copy-start.11 = (f32[4096]{0:T(1024)S(1)}, f32[4096]{0:T(1024)}, u32[]{:S(2)}) copy-start(f32[4096]{0:T(1024)} %copy-done.10) | copy-start | bytes 49156
  347.4 33.2 %copy-start.13 = (f32[4096]{0:T(1024)S(1)}, f32[4096]{0:T(1024)}, u32[]{:S(2)}) copy-start(f32[4096]{0:T(1024)} %copy-done.12) | copy-start | bytes 49156
  413.4 231.2 %reduce-scatter.17.cloned.1.call-start = ((), (), s32[]{:S(2)}) async-start(), calls=%async_computation.11 | async-start | bytes 5242880 | tf_op jit(solution)/shard_map/reduce_scatter | solution.py:43
  458.8 24.6 %copy-start.17 = (f32[4096]{0:T(1024)S(1)}, f32[4096]{0:T(1024)}, u32[]{:S(2)}) copy-start(f32[4096]{0:T(1024)} %copy-done.16) | copy-start | bytes 49156
  458.8 185.8 %reduce-scatter.11.cloned.1.call-start = ((), (), s32[]{:S(2)}) async-start(), calls=%async_computation.8 | async-start | bytes 5242880 | tf_op jit(solution)/shard_map/reduce_scatter | solution.py:43
  458.9 24.6 %copy-start = (bf16[1,4096,512]{1,2,0:T(8,128)(2,1)S(1)}, bf16[1,4096,512]{1,2,0:T(8,128)(2,1)}, u32[]{:S(2)}) copy-start(bf16[1,4096,512]{1,2,0:T(8,128)(2,1)} %copy.20) | copy-start | bytes 12582916
  521.1 123.5 %reduce-scatter.13.cloned.1.call-start = ((), (), s32[]{:S(2)}) async-start(), calls=%async_computation.9 | async-start | bytes 5242880 | tf_op jit(solution)/shard_map/reduce_scatter | solution.py:43
  561.1 103.1 %reduce-scatter.7.cloned.1.call-start = ((), (), s32[]{:S(2)}) async-start(), calls=%async_computation.6 | async-start | bytes 5242880 | tf_op jit(solution)/shard_map/reduce_scatter | solution.py:43
  620.2 90.8 %reduce-scatter.9.cloned.1.call-start = ((), (), s32[]{:S(2)}) async-start(), calls=%async_computation.7 | async-start | bytes 5242880 | tf_op jit(solution)/shard_map/reduce_scatter | solution.py:43
  644.5 281.8 %all-reduce.3.cloned.1.call-start = ((), (), s32[]{:S(2)}) async-start(), calls=%async_computation.18 | async-start | bytes 12582912 | tf_op jit(solution)/shard_map/psum | solution.py:43
  711.0 232.8 %copy-start.2 = (bf16[2,1024,512]{2,1,0:T(8,128)(2,1)S(1)}, bf16[2,1024,512]{2,1,0:T(8,128)(2,1)}, u32[]{:S(2)}) copy-start(bf16[2,1024,512]{2,1,0:T(8,128)(2,1)} %param.15) | copy-start | bytes 6291460
  943.8 8.4 copy-start.3
  943.8 8.4 copy-start.4
  943.8 8.4 copy-start.7
  (7 other events, 28.4 us)
Sparse Core Ops, SparseCore 0:
  10.4 37.0 all-gather.12
  49.7 34.2 all-gather.14
  86.1 34.2 all-gather.16
  122.4 34.2 all-gather.20
  158.7 34.2 all-gather.22
  195.0 34.2 all-gather.18
  413.5 43.8 reduce-scatter.14
  460.4 43.8 reduce-scatter.16
  521.2 43.8 reduce-scatter.10
  568.0 43.8 reduce-scatter.12
  620.3 43.8 reduce-scatter.6
  667.1 43.8 reduce-scatter.8
  716.0 210.2 all-reduce.2
where the time goes:
time: 981 us; the launch traced here: 972 us
  matrix products  575 us (59%)
  waiting for transfers between devices  310 us (32%)
  other arithmetic  39.7 us (4%)
  local copies, waits for them, and re-layouts  23.8 us (2%)
  between operations  17.2 us (2%)
    dot_general x5, matrix products, layer(): gate = jnp.dot(a, w['w_gate'], preferred_element_type=jnp.float32)  225 us
    psum x1, waiting for transfers between devices, summed(): lax.psum(lax.psum_scatter(term, 's', scatter_dimension=0, tiled=True), 'r')  215 us
    dot_general x5, matrix products, layer(): up = jnp.dot(a, w['w_up'], preferred_element_type=jnp.float32)  206 us
    dot_general x5, matrix products, matmul(): jnp.dot(a, w, preferred_element_type=jnp.float32).astype(jnp.bfloat16)  143 us
    reduce_scatter x6, waiting for transfers between devices, summed(): lax.psum_scatter(term, 's', scatter_dimension=0, tiled=True)  66.4 us
    all_gather x6, waiting for transfers between devices, fetched(): lax.all_gather(w[number], 's', axis=0, tiled=True)  26.7 us
    convert_element_type x2, other arithmetic, adamw(): return ((w - 0.02 * step).astype(jnp.bfloat16), m, v)  21.6 us
  transfers between devices with their start and end apart: 13, of which 6 were waited for; matrix products, arithmetic and copies ran while one was open for 43% of the time, Pallas kernels for 0%

commit v1 on v0

v1 whole, which is shorter than its diff:
```python
import functools

import jax
import jax.numpy as jnp
from jax import lax
from jax.experimental import pallas as pl
from jax.experimental.pallas import tpu as pltpu
from jax.sharding import PartitionSpec as P

MESH = pl.DeviceIdType.MESH
CHUNKS, CORES, XS, YS, ZS, OWNERS = 8, 2, 2, 2, 4, 4
f32, bf16 = jnp.float32, jnp.bfloat16


def dotn(a, b):
    return jnp.dot(a, b, preferred_element_type=f32)


def dott(a, b):
    return lax.dot_general(a, b, (((1,), (1,)), ((), ())), preferred_element_type=f32)


def dot0(a, b):
    return lax.dot_general(a, b, (((0,), (0,)), ((), ())), preferred_element_type=f32)


def kernel(
    sizes,
    x_hbm, dy_hbm, wg_hbm, wu_hbm, wd_hbm,
    gg_out, gu_out, gd_out, wbuf, a0_hbm,
    A, DH, H, total, W, act_s, du_s, dg_s, accs,
    sb0, rb0, own0, sb1, rb1, own1, sb2, rb2, own2, sb3, rb3, own3, gfin,
    in_sem, w_sem, out_sem,
    ws_send, wf_send, w_recv,
    s0, r0, s1, r1, s2, r2, s3, r3, s4, r4,
):
    T, D, F, Tt, rb, cb = sizes
    R = D // OWNERS
    HALF, QUARTER = R // YS, R // (YS * ZS)
    nt = T // Tt
    per = nt // 2
    me_r, me_s = lax.axis_index("r"), lax.axis_index("s")
    core, mx = lax.rem(me_s, CORES), me_s // CORES
    my, mz = me_r // ZS, lax.rem(me_r, ZS)
    partner = mx * CORES + 1 - core
    across = (1 - mx) * CORES + core
    to_partner = {"r": me_r, "s": partner}
    to_across = {"r": me_r, "s": across}
    to_y = {"r": (1 - my) * ZS + mz, "s": me_s}

    def remote(src, dst, send, recv, where):
        return pltpu.make_async_remote_copy(src, dst, send, recv, device_id=where, device_id_type=MESH)

    def rows(owner):
        return pl.ds(pl.multiple_of(owner * R, R), R)

    def own_pieces(l, j, into):
        wide = F // OWNERS
        for m, w in ((0, wg_hbm), (1, wu_hbm)):
            for o in range(OWNERS):
                cols = pl.ds(pl.multiple_of(o * wide * CHUNKS + j * wide, wide), wide)
                yield w.at[l, :, cols], into.at[m, rows(me_s), o * wide : (o + 1) * wide]
        yield wd_hbm.at[l, rows(j), :], into.at[2, rows(me_s), :]

    def send_own(c):
        l, j = c // CHUNKS, lax.rem(c, CHUNKS)
        for src, dst in own_pieces(l, j, wbuf.at[l, j]):
            remote(src, dst, ws_send.at[0, c], w_recv.at[0, c], to_across).start()
        for src, dst in own_pieces(l, j, wbuf.at[l, j]):
            remote(src, dst, ws_send.at[1, c], w_recv.at[1, c], to_partner).start()

    def package(c, owner):
        return wbuf.at[c // CHUNKS, lax.rem(c, CHUNKS), :, rows(owner), :]

    def wait_package(kind, c, owner):
        remote(package(c, owner), package(c, owner), wf_send.at[c], w_recv.at[kind, c], to_partner).wait_recv()

    def forward(c):
        wait_package(0, c, across)
        remote(package(c, across), package(c, across), wf_send.at[c], w_recv.at[2, c], to_partner).start()

    def load(n):
        slot = lax.rem(n, 2)
        l, j = lax.rem(n // CHUNKS, 2), lax.rem(n, CHUNKS)

        @pl.when(n < 2 * CHUNKS)
        def _():
            wait_package(1, n, partner)
            wait_package(2, n, (1 - mx) * CORES + 1 - core)

        for src, dst in own_pieces(l, j, W.at[slot]):
            pltpu.make_async_copy(src, dst, w_sem.at[slot]).start()
        for k in range(1, OWNERS):
            o = lax.rem(me_s + k, OWNERS)
            pltpu.make_async_copy(wbuf.at[l, j, :, rows(o), :], W.at[slot, :, rows(o), :], w_sem.at[slot]).start()

    def wait_load(n):
        slot = lax.rem(n, 2)
        pltpu.make_async_copy(wbuf.at[0, 0], W.at[slot], w_sem.at[slot]).wait()

    def g0(q):
        for m in range(3):
            for xx in range(XS):
                sb0[m, xx] = accs[m, rows(xx * CORES + 1 - core), :].astype(bf16)
        for m in range(3):
            for xx in range(XS):
                own0[m, xx] = accs[m, rows(xx * CORES + core), :]
        c0(q).start()

    def c0(q):
        return remote(sb0, rb0.at[lax.rem(q, 2)], s0, r0.at[lax.rem(q, 2)], to_partner)

    def g1(q):
        c0(q).wait()
        slot = lax.rem(q, 2)
        for m in range(3):
            sb1[m] = (own0[m, 1 - mx] + rb0[slot, m, 1 - mx].astype(f32)).astype(bf16)
        for m in range(3):
            own1[m] = own0[m, mx] + rb0[slot, m, mx].astype(f32)
        c1(q).start()

    def c1(q):
        return remote(sb1, rb1.at[lax.rem(q, 2)], s1, r1.at[lax.rem(q, 2)], to_across)

    def half(h):
        return pl.ds(pl.multiple_of(h * HALF, HALF), HALF)

    def g2(q):
        c1(q).wait()
        slot = lax.rem(q, 2)
        for m in range(3):
            sb2[m] = (own1[m, half(1 - my), :] + rb1[slot, m, half(1 - my), :].astype(f32)).astype(bf16)
        for m in range(3):
            own2[m] = own1[m, half(my), :] + rb1[slot, m, half(my), :].astype(f32)
        c2(q).start()

    def c2(q):
        return remote(sb2, rb2.at[lax.rem(q, 2)], s2, r2.at[lax.rem(q, 2)], to_y)

    def quarter(z):
        return pl.ds(pl.multiple_of(z * QUARTER, QUARTER), QUARTER)

    def c3(q, k):
        where = {"r": my * ZS + lax.rem(mz + 1 + k, ZS), "s": me_s}
        return remote(sb3.at[k], rb3.at[lax.rem(q, 2), k], s3.at[k], r3.at[lax.rem(q, 2), k], where)

    def g3(q):
        c2(q).wait()
        slot = lax.rem(q, 2)
        for k in range(ZS - 1):
            z = lax.rem(mz + 1 + k, ZS)
            for m in range(3):
                sb3[k, m] = (own2[m, quarter(z), :] + rb2[slot, m, quarter(z), :].astype(f32)).astype(bf16)
        for m in range(3):
            own3[m] = own2[m, quarter(mz), :] + rb2[slot, m, quarter(mz), :].astype(f32)
        for k in range(ZS - 1):
            c3(q, k).start()

    mine = pl.ds(pl.multiple_of(my * HALF + mz * QUARTER, QUARTER), QUARTER)

    def c4(q, k):
        part = gfin.at[q, :, mine, :]
        where = {"r": lax.rem(me_r + 1 + k, YS * ZS), "s": me_s}
        return remote(part, part, s4.at[q], r4.at[q], where)

    def all4(q):
        others = gfin.at[q, :, : R - QUARTER, :]
        return remote(others, others, s4.at[q], r4.at[q], to_y)

    def g4(q):
        slot = lax.rem(q, 2)
        for k in range(ZS - 1):
            c3(q, k).wait()
        for m in range(3):
            v = own3[m]
            for k in range(ZS - 1):
                v += rb3[slot, k, m].astype(f32)
            gfin[q, m, mine, :] = v.astype(bf16)
        for k in range(YS * ZS - 1):
            c4(q, k).start()

    def stores(q):
        l, j = 1 - q // CHUNKS, lax.rem(q, CHUNKS)
        wide = F // OWNERS
        for m, g in ((0, gg_out), (1, gu_out)):
            for o in range(OWNERS):
                cols = pl.ds(pl.multiple_of(o * wide * CHUNKS + j * wide, wide), wide)
                yield pltpu.make_async_copy(gfin.at[q, m, :, o * wide : (o + 1) * wide], g.at[l, :, cols], out_sem.at[q])
        yield pltpu.make_async_copy(gfin.at[q, 2], gd_out.at[l, rows(j), :], out_sem.at[q])

    def store(q):
        all4(q).wait()
        for copy in stores(q):
            copy.start()

    def when(test, what, q):
        pl.when(test)(lambda: what(q))

    last = 2 * CHUNKS

    def exchange(q, b):
        def at(stage, back, what):
            when((b == stage) & (q >= back) & (q < last + back), what, q - back)

        at(0, 4, store)
        at(0, 3, g4)
        at(0, 2, g2)
        at(0, 1, g0)
        at(1, 1, g1)
        at(2, 2, g3)

    def normed(wide):
        scale = lax.rsqrt(jnp.mean(wide * wide, -1, keepdims=True) + 1e-6)
        return (wide * scale).astype(bf16)

    def tile(t, n=Tt):
        return pl.ds(pl.multiple_of(t * n, n), n)

    def first(wslot, t, slot, backward, r, c):
        s = pl.ds(pl.multiple_of(t * Tt + r * rb, rb), rb)
        rs, cs = slice(r * rb, (r + 1) * rb), slice(c * cb, (c + 1) * cb)
        a = A[s, :]
        g = dotn(a, W[wslot, 0, :, cs])
        u = dotn(a, W[wslot, 1, :, cs])
        h = 0.5 * g
        th = jnp.tanh(h)
        silu = h * th + h
        if not backward:
            act_s[slot, rs, cs] = (silu * u).astype(bf16)
            return
        d = dott(DH[s, :], W[wslot, 2, cs, :]).astype(bf16).astype(f32)
        sig = 0.5 * th + 0.5
        act_s[slot, rs, cs] = (silu * u).astype(bf16)
        du_s[slot, rs, cs] = (d * silu).astype(bf16)
        dg_s[slot, rs, cs] = (d * u * (sig * (1.0 + g - silu))).astype(bf16)

    def second(wslot, t, slot, backward, input_too, begin, piece):
        s = tile(t)
        if not backward:
            total[s, :] += dotn(act_s[slot], W[wslot, 2])
            return
        if piece == 3:
            total[s, :] += dott(dg_s[slot], W[wslot, 0]) + dott(du_s[slot], W[wslot, 1])
            return
        if piece == 2:
            new = dot0(act_s[slot], DH[s, :])
        else:
            new = dot0(A[s, :], (dg_s, du_s)[piece][slot])
        if begin:
            accs[piece] = jnp.where(t == 0, 0.0, accs[piece]) + new
        else:
            accs[piece] += new

    blocks = [(r, c) for r in range(Tt // rb) for c in range(F // cb)]

    def together(w1, t1, slot1, w2, t2, slot2, backward, input_too, begin):
        pieces = list(range(4 if input_too else 3)) if backward else [0]
        done = 0
        for k, block in enumerate(blocks):
            first(w1, t1, slot1, backward, *block)
            while done < (k + 1) * len(pieces) // len(blocks):
                second(w2, t2, slot2, backward, input_too, begin, pieces[done])
                done += 1

    def phase(base, backward, input_too):
        for block in blocks:
            first(lax.rem(base, 2), 0, 0, backward, *block)

        def step(i, _):
            n, b = base + i // per, lax.rem(i, per)
            if backward:
                exchange(n - CHUNKS, b)
            if base < 2 * CHUNKS:
                when((b == 0) & (n + 4 < 2 * CHUNKS), send_own, n + 4)
                when((b == 0) & (n + 1 < 2 * CHUNKS), forward, n + 1)
            when((b == 1) & (n + 1 < 3 * CHUNKS), load, n + 1)
            when((b == per - 1) & (n + 1 < 3 * CHUNKS), wait_load, n + 1)
            w = lax.rem(n, 2)
            t = 2 * b
            together(w, t + 1, 1, w, t, 0, backward, input_too, True)
            over = b == per - 1
            together(jnp.where(over, 1 - w, w), jnp.where(over, 0, t + 2), 0, w, t + 1, 1, backward, input_too, False)
            return 0

        lax.fori_loop(0, per * CHUNKS, step, 0)

    barrier = pltpu.get_barrier_semaphore()
    peers = [to_partner, to_across] + [{"r": lax.rem(me_r + k, YS * ZS), "s": me_s} for k in range(1, YS * ZS)]
    for peer in peers:
        pl.semaphore_signal(barrier, inc=1, device_id=peer, device_id_type=MESH)
    load_x = pltpu.make_async_copy(x_hbm, H, in_sem.at[0])
    load_dy = pltpu.make_async_copy(dy_hbm, DH, in_sem.at[1])
    load_x.start()
    load_dy.start()
    pl.semaphore_wait(barrier, len(peers))
    lax.fori_loop(0, 4, lambda c, _: (send_own(c), 0)[1], 0)
    load_x.wait()

    def begin(t, _):
        s = tile(t, rb)
        A[s, :] = normed(H[s, :].astype(f32))
        total[s, :] = jnp.zeros((rb, D), f32)
        return 0

    lax.fori_loop(0, T // rb, begin, 0)
    save_a = pltpu.make_async_copy(A, a0_hbm, in_sem.at[0])
    save_a.start()
    forward(0)
    load(0)
    wait_load(0)
    phase(0, False, False)
    save_a.wait()
    load_dy.wait()

    def between(t, _):
        s = tile(t, rb)
        h = (H[s, :].astype(f32) + total[s, :].astype(bf16).astype(f32)).astype(bf16)
        H[s, :] = h
        A[s, :] = normed(h.astype(f32))
        total[s, :] = jnp.zeros((rb, D), f32)
        return 0

    lax.fori_loop(0, T // rb, between, 0)
    phase(CHUNKS, True, True)
    load_a = pltpu.make_async_copy(a0_hbm, A, in_sem.at[0])
    load_a.start()

    def back(t, _):
        s = tile(t, rb)
        wide = H[s, :].astype(f32)
        da = total[s, :].astype(bf16).astype(f32)
        scale = lax.rsqrt(jnp.mean(wide * wide, -1, keepdims=True) + 1e-6)
        along = jnp.sum(da * wide, -1, keepdims=True) * (scale * scale * scale * (1.0 / D))
        dn = (da * scale - wide * along).astype(bf16).astype(f32)
        DH[s, :] = (DH[s, :].astype(f32) + dn).astype(bf16)
        return 0

    lax.fori_loop(0, T // rb, back, 0)
    load_a.wait()
    phase(2 * CHUNKS, True, False)

    def drain(i, _):
        exchange(last + i // per, lax.rem(i, per))
        return 0

    lax.fori_loop(0, 4 * per, drain, 0)

    def finish(q, _):
        for copy in stores(q):
            copy.wait()
        l, j = q // CHUNKS, lax.rem(q, CHUNKS)
        two = wbuf.at[l, j, :, : R, :]
        for k in range(2):
            remote(two, two, ws_send.at[k, q], w_recv.at[0, q], to_partner).wait_send()
        remote(two, two, wf_send.at[q], w_recv.at[0, q], to_partner).wait_send()
        return 0

    lax.fori_loop(0, last, finish, 0)


def gradients_of(x, dy, w_gate, w_up, w_down, tiles=(512, 256, 256), vmem=63 * 2**20):
    T, D = x.shape
    F = w_gate.shape[2] // CHUNKS
    Tt, rb, cb = tiles
    R = D // OWNERS
    H, Q = R // YS, R // (YS * ZS)
    n = 2 * CHUNKS
    vm = pltpu.VMEM
    dma, any_ = pltpu.SemaphoreType.DMA, pl.BlockSpec(memory_space=pl.ANY)
    shape = jax.ShapeDtypeStruct
    outs = pl.pallas_call(
        functools.partial(kernel, (T, D, F, Tt, rb, cb)),
        in_specs=[any_] * 5,
        out_specs=[any_] * 5,
        out_shape=[shape(w.shape, bf16) for w in (w_gate, w_up, w_down)]
        + [shape((2, CHUNKS, 3, D, F), bf16), shape((T, D), bf16)],
        scratch_shapes=[
            vm((T, D), bf16), vm((T, D), bf16), vm((T, D), bf16), vm((T, D), f32),
            vm((2, 3, D, F), bf16), vm((2, Tt, F), bf16), vm((2, Tt, F), bf16), vm((2, Tt, F), bf16), vm((3, D, F), f32),
            vm((3, XS, R, F), bf16), vm((2, 3, XS, R, F), bf16), vm((3, XS, R, F), f32),
            vm((3, R, F), bf16), vm((2, 3, R, F), bf16), vm((3, R, F), f32),
            vm((3, H, F), bf16), vm((2, 3, H, F), bf16), vm((3, H, F), f32),
            vm((ZS - 1, 3, Q, F), bf16), vm((2, ZS - 1, 3, Q, F), bf16), vm((3, Q, F), f32),
            vm((n, 3, R, F), bf16),
            dma((2,)), dma((2,)), dma((n,)),
            dma((2, n)), dma((n,)), dma((3, n)),
            dma, dma((2,)), dma, dma((2,)), dma, dma((2,)), dma((ZS - 1,)), dma((2, ZS - 1)), dma((n,)), dma((n,)),
        ],
        compiler_params=pltpu.CompilerParams(collective_id=0, has_side_effects=True, vmem_limit_bytes=vmem),
    )(x, dy, w_gate, w_up, w_down)
    return outs[:3]


def adamw(w, m, v, g):
    m = 0.9 * m + 0.1 * g
    v = 0.95 * v + 0.05 * g * g
    step = m * lax.rsqrt(v + 1e-8) + 0.1 * w
    return (w - 0.02 * step).astype(bf16), m, v


def clipped(gradients, sum_of_squares, count):
    factor = jnp.minimum(1.0, 0.5 * lax.rsqrt(sum_of_squares / count + 1e-30))
    return [g * factor for g in gradients]


def solution(mesh, **options):
    def step(x, dy, *arrays):
        weights, m, v = (arrays[i : i + 3] for i in (0, 3, 6))
        gradients = [g.astype(f32) for g in gradients_of(x[0], dy[0], *weights, **options)]
        squares = lax.psum(sum(jnp.sum(g * g) for g in gradients), "s")
        gradients = clipped(gradients, squares, lax.psum(1, "s") * sum(g.size for g in gradients))
        new = [adamw(w.astype(f32), m, v, g) for w, m, v, g in zip(weights, m, v, gradients, strict=True)]
        return tuple(one[which] for which in range(3) for one in new)

    states, cut = P(("rep", "r", "s"), None, None), P(None, "s", None)
    return jax.shard_map(
        step,
        mesh=mesh,
        in_specs=(states, states) + (cut,) * 9,
        out_specs=(P("rep", "s", None),) * 9,
        check_vma=False,
    )
```

time: 981 us -> 477 us (0.49)
  matrix products: 575 us -> 0 us
  Pallas kernels: 0 us -> 434 us
  waiting for transfers between devices: 310 us -> 0 us
  local copies, waits for them, and re-layouts: 23.8 us -> 0.02 us
  between operations: 17.2 us -> 3.34 us
    dot_general x15 -> x0, matrix products: 575 us -> none  [the longest x5 225 us: layer(): gate = jnp.dot(a, w['w_gate'], preferred_element_type=jnp.float32)]
    pallas_call x0 -> x1, Pallas kernels: none -> 434 us  [gradients_of(): pl.pallas_call(functools.partial(kernel, (T, D, F, Tt, rb, cb)), in_specs...]
    psum x1 -> x0, waiting for transfers between devices: 215 us -> none  [summed(): lax.psum(lax.psum_scatter(term, 's', scatter_dimension=0, tiled=True), 'r')]
    reduce_scatter x6 -> x0, waiting for transfers between devices: 66.4 us -> none  [summed(): lax.psum_scatter(term, 's', scatter_dimension=0, tiled=True)]
    all_gather x6 -> x0, waiting for transfers between devices: 26.7 us -> none  [fetched(): lax.all_gather(w[number], 's', axis=0, tiled=True)]
    unnamed x38 -> x6, local copies, waits for them, and re-layouts: 16 us -> 0.02 us
  transfers between devices with their start and end apart: 13 -> 0, of which waited for: 6 -> 0; matrix products, arithmetic and copies ran while one was open for 43% -> 0% of each run, Pallas kernels for 0% -> 0%
where the time goes in v1:
time: 477 us
  Pallas kernels  434 us (91%)
  other arithmetic  33.7 us (7%)
  blocking collectives  6.27 us (1%)
    pallas_call x1, Pallas kernels, gradients_of(): pl.pallas_call(functools.partial(kernel, (T, D, F, Tt, rb, cb)), in_specs...  434 us
    convert_element_type x2, other arithmetic, adamw(): return ((w - 0.02 * step).astype(bf16), m, v)  23.7 us
    reduce_sum x3, other arithmetic, step(): squares = lax.psum(sum((jnp.sum(g * g) for g in gradients)), 's')  9.97 us

profile of v1, /device:TPU:0, one launch (start us, length us, event | category | flops | bytes accessed | tf_op | source)
XLA Modules:
  0.0 477.1 jit_solution(4056640321158354153)
XLA Ops:
  0.6 433.8 %shard_map.178 = (bf16[2,128,4096]{2,1,0:T(8,128)(2,1)}, bf16[2,128,4096]{2,1,0:T(8,128)(2,1)}, bf16[2,1024,512]{2,1,0:T(8,128)(2,1)}, bf16[2,8,3,512,512]{4,3,2,1,0:T(8,128)(2,1)}, bf16[4096,512]{1,0:T(8,128)(2,1)}) custom-call(bf16[4096,512]{1,0:T(8,128)(2,1)} %bitcast.2, bf16[4096,512]{1,0:T(8,128)(2,1)} %bitcast.3, bf16[2,128,4096]{2,1,0:T(8,128)(2,1)} %wg_hbm.1, ...), custom_call_target="tpu_custom_call" | custom-call | tf_op jit(solution)/shard_map/pallas_call | solution.py:371
  434.5 0.0 copy-start
  434.5 3.4 fusion.10
  437.9 3.3 fusion.9
  442.5 3.3 fusion.11
  446.4 6.3 %psum.7 = f32[]{:T(128)} all-reduce(f32[]{:T(128)S(6)} %add.51), channel_id=1, replica_groups=mesh['rep'=1,'r'=8,'s'=4] {'s'}, use_global_device_ids=true, to_apply=%region_3.0 | all-reduce | flops 1 | bytes 8 | tf_op jit(solution)/shard_map/psum | solution.py:410
  453.4 0.0 copy-done
  453.4 0.0 copy-start.1
  453.4 0.0 copy-start.2
  453.4 16.8 %fusion.8 = (bf16[2,128,4096]{2,1,0:T(8,128)(2,1)}, f32[2,128,4096]{2,1,0:T(8,128)}, f32[2,128,4096]{2,1,0:T(8,128)}, bf16[2,128,4096]{2,1,0:T(8,128)(2,1)}, f32...) fusion(bf16[2,128,4096]{2,1,0:T(8,128)(2,1)S(1)} %copy-done, f32[]{:T(128)S(6)} %min_shard_map.3, ...), kind=kLoop, calls=%fused_computation.23 | loop fusion | flops 35651584 | bytes 46137348 | tf_op jit(solution)/shard_map/convert_element_type | solution.py:398
  470.2 0.0 copy-done.1
  470.2 0.0 copy-done.2
  470.2 6.9 %fusion.17 = (bf16[2,1024,512]{2,1,0:T(8,128)(2,1)}, f32[2,1024,512]{2,1,0:T(8,128)}, f32[2,1024,512]{2,1,0:T(8,128)}) fusion(bf16[2,1024,512]{2,1,0:T(8,128)(2,1)S(1)} %copy-done.1, f32[]{:T(128)S(6)} %min_shard_map.3, bf16[2,1024,512]{2,1,0:T(8,128)(2,1)S(1)} %copy-done.2, f32[2,1024,512]{2,1,0:T(8,128)} %param.21, f32[2,1024,512]{2,1,0:T(8,128)} %param.18), kind=kLoop, calls=%fused_computation.32 | loop fusion | flops 17825792 | bytes 23068676 | tf_op jit(solution)/shard_map/convert_element_type | solution.py:398
Async XLA Ops:
  434.5 18.9 %copy-start = (bf16[2,128,4096]{2,1,0:T(8,128)(2,1)S(1)}, bf16[2,128,4096]{2,1,0:T(8,128)(2,1)}, u32[]{:S(2)}) copy-start(bf16[2,128,4096]{2,1,0:T(8,128)(2,1)} %wg_hbm.1) | copy-start | bytes 6291460
  453.4 16.8 %copy-start.1 = (bf16[2,1024,512]{2,1,0:T(8,128)(2,1)S(1)}, bf16[2,1024,512]{2,1,0:T(8,128)(2,1)}, u32[]{:S(2)}) copy-start(bf16[2,1024,512]{2,1,0:T(8,128)(2,1)} %wd_hbm.1) | copy-start | bytes 6291460
  453.4 16.8 %copy-start.2 = (bf16[2,1024,512]{2,1,0:T(8,128)(2,1)S(1)}, bf16[2,1024,512]{2,1,0:T(8,128)(2,1)}, u32[]{:S(2)}) copy-start(bf16[2,1024,512]{2,1,0:T(8,128)(2,1)} %get-tuple-element.14) | copy-start | bytes 6291460

commit v2 on v1

v2 whole, which is shorter than its diff:
```python
import functools

import jax
import jax.numpy as jnp
from jax import lax
from jax.experimental import pallas as pl
from jax.experimental.pallas import tpu as pltpu
from jax.sharding import PartitionSpec as P

MESH = pl.DeviceIdType.MESH
CHUNKS, CORES, XS, YS, ZS, OWNERS = 8, 2, 2, 2, 4, 4
f32, bf16 = jnp.float32, jnp.bfloat16

EARLY = ((1, 0), (1, 1), (1, 2), (2, 0), (2, 1))


def dotn(a, b):
    return jnp.dot(a, b, preferred_element_type=f32)


def dott(a, b):
    return lax.dot_general(a, b, (((1,), (1,)), ((), ())), preferred_element_type=f32)


def dot0(a, b):
    return lax.dot_general(a, b, (((0,), (0,)), ((), ())), preferred_element_type=f32)


def kernel(
    sizes,
    x_hbm, dy_hbm, wg_hbm, wu_hbm, wd_hbm, *refs,
):
    early, refs = refs[: len(EARLY)], refs[len(EARLY) :]
    kernel_(sizes, x_hbm, dy_hbm, wg_hbm, wu_hbm, wd_hbm, early, refs[4 : 4 + len(EARLY)], *refs[:4], *refs[4 + len(EARLY) :])


def kernel_(
    sizes,
    x_hbm, dy_hbm, wg_hbm, wu_hbm, wd_hbm, early, early_out, gfin, factor, wbuf, a0_hbm,
    A, DH, H, total, W, act_s, du_s, dg_s, accs,
    sb0, rb0, own0, sb1, rb1, own1, sb2, rb2, own2, sb3, rb3, own3, piece, squares, over_r, over_s,
    in_sem, early_sem, w_sem, out_sem,
    ws_send, wf_send, w_recv,
    s0, r0, s1, r1, s2, r2, s3, r3, s4, r4, s5, r5, sn, rn, sm, rm,
):
    T, D, F, Tt, rb, cb, LANES = sizes
    COUNT = 2 * CHUNKS * 3 * D * F
    R = D // OWNERS
    HALF, QUARTER = R // YS, R // (YS * ZS)
    nt = T // Tt
    per = nt // 2
    me_r, me_s = lax.axis_index("r"), lax.axis_index("s")
    core, mx = lax.rem(me_s, CORES), me_s // CORES
    my, mz = me_r // ZS, lax.rem(me_r, ZS)
    partner = mx * CORES + 1 - core
    across = (1 - mx) * CORES + core
    to_partner = {"r": me_r, "s": partner}
    to_across = {"r": me_r, "s": across}
    to_y = {"r": (1 - my) * ZS + mz, "s": me_s}

    def remote(src, dst, send, recv, where):
        return pltpu.make_async_remote_copy(src, dst, send, recv, device_id=where, device_id_type=MESH)

    def rows(owner):
        return pl.ds(pl.multiple_of(owner * R, R), R)

    def own_pieces(l, j, into):
        wide = F // OWNERS
        for m, w in ((0, wg_hbm), (1, wu_hbm)):
            for o in range(OWNERS):
                cols = pl.ds(pl.multiple_of(o * wide * CHUNKS + j * wide, wide), wide)
                yield w.at[l, :, cols], into.at[m, rows(me_s), o * wide : (o + 1) * wide]
        yield wd_hbm.at[l, rows(j), :], into.at[2, rows(me_s), :]

    def send_own(c):
        l, j = c // CHUNKS, lax.rem(c, CHUNKS)
        for src, dst in own_pieces(l, j, wbuf.at[l, j]):
            remote(src, dst, ws_send.at[0, c], w_recv.at[0, c], to_across).start()
        for src, dst in own_pieces(l, j, wbuf.at[l, j]):
            remote(src, dst, ws_send.at[1, c], w_recv.at[1, c], to_partner).start()

    def package(c, owner):
        return wbuf.at[c // CHUNKS, lax.rem(c, CHUNKS), :, rows(owner), :]

    def wait_package(kind, c, owner):
        remote(package(c, owner), package(c, owner), wf_send.at[c], w_recv.at[kind, c], to_partner).wait_recv()

    def forward(c):
        wait_package(0, c, across)
        remote(package(c, across), package(c, across), wf_send.at[c], w_recv.at[2, c], to_partner).start()

    def load(n):
        slot = lax.rem(n, 2)
        l, j = lax.rem(n // CHUNKS, 2), lax.rem(n, CHUNKS)

        @pl.when(n < 2 * CHUNKS)
        def _():
            wait_package(1, n, partner)
            wait_package(2, n, (1 - mx) * CORES + 1 - core)

        for src, dst in own_pieces(l, j, W.at[slot]):
            pltpu.make_async_copy(src, dst, w_sem.at[slot]).start()
        for k in range(1, OWNERS):
            o = lax.rem(me_s + k, OWNERS)
            pltpu.make_async_copy(wbuf.at[l, j, :, rows(o), :], W.at[slot, :, rows(o), :], w_sem.at[slot]).start()

    def wait_load(n):
        slot = lax.rem(n, 2)
        pltpu.make_async_copy(wbuf.at[0, 0], W.at[slot], w_sem.at[slot]).wait()

    def c0(q, m):
        slot = lax.rem(q, 2)
        return remote(sb0.at[m], rb0.at[slot, m], s0.at[m], r0.at[slot, m], to_partner)

    def g0(q, m):
        for xx in range(XS):
            sb0[m, xx] = accs[m, rows(xx * CORES + 1 - core), :].astype(bf16)
        for xx in range(XS):
            own0[m, xx] = accs[m, rows(xx * CORES + core), :]
        c0(q, m).start()

    def c1(q, m):
        slot = lax.rem(q, 2)
        return remote(sb1.at[m], rb1.at[slot, m], s1.at[m], r1.at[slot, m], to_across)

    def g1(q, m):
        c0(q, m).wait()
        slot = lax.rem(q, 2)
        sb1[m] = (own0[m, 1 - mx] + rb0[slot, m, 1 - mx].astype(f32)).astype(bf16)
        own1[m] = own0[m, mx] + rb0[slot, m, mx].astype(f32)
        c1(q, m).start()

    def half(h):
        return pl.ds(pl.multiple_of(h * HALF, HALF), HALF)

    def c2(q, m):
        slot = lax.rem(q, 2)
        return remote(sb2.at[m], rb2.at[slot, m], s2.at[m], r2.at[slot, m], to_y)

    def g2(q, m):
        c1(q, m).wait()
        slot = lax.rem(q, 2)
        sb2[m] = (own1[m, half(1 - my), :] + rb1[slot, m, half(1 - my), :].astype(f32)).astype(bf16)
        own2[m] = own1[m, half(my), :] + rb1[slot, m, half(my), :].astype(f32)
        c2(q, m).start()

    def quarter(z):
        return pl.ds(pl.multiple_of(z * QUARTER, QUARTER), QUARTER)

    def c3(q, m, k):
        where = {"r": my * ZS + lax.rem(mz + 1 + k, ZS), "s": me_s}
        slot = lax.rem(q, 2)
        return remote(sb3.at[m, k], rb3.at[slot, m, k], s3.at[m, k], r3.at[slot, m, k], where)

    def g3(q, m):
        c2(q, m).wait()
        slot = lax.rem(q, 2)
        for k in range(ZS - 1):
            z = lax.rem(mz + 1 + k, ZS)
            sb3[m, k] = (own2[m, quarter(z), :] + rb2[slot, m, quarter(z), :].astype(f32)).astype(bf16)
        own3[m] = own2[m, quarter(mz), :] + rb2[slot, m, quarter(mz), :].astype(f32)
        for k in range(ZS - 1):
            c3(q, m, k).start()

    mine = pl.ds(pl.multiple_of(my * HALF + mz * QUARTER, QUARTER), QUARTER)

    def to_peer(k):
        return {"r": lax.rem(me_r + 1 + k, YS * ZS), "s": me_s}

    def c4(q, m, k):
        where = {"r": my * ZS + lax.rem(mz + 1 + k, ZS), "s": me_s}
        return remote(piece.at[q, m], gfin.at[q, m, mine, :], s4.at[q, m], r4.at[q, m], where)

    def c4_here(q, m):
        return pltpu.make_async_copy(piece.at[q, m], gfin.at[q, m, mine, :], out_sem.at[q, m])

    def g4(q, m):
        slot = lax.rem(q, 2)
        for k in range(ZS - 1):
            c3(q, m, k).wait()
        v = own3[m]
        for k in range(ZS - 1):
            v += rb3[slot, m, k].astype(f32)
        v = v.astype(bf16)
        piece[q, m] = v
        v = v.astype(f32)
        squares[...] += sum(v[:, i : i + LANES] * v[:, i : i + LANES] for i in range(0, F, LANES))
        for k in range(ZS - 1):
            c4(q, m, k).start()
        c4_here(q, m).start()

    def c5(q, m):
        part = gfin.at[q, m, half(my), :]
        return remote(part, part, s5.at[q, m], r5.at[q, m], to_y)

    def g5(q, m):
        others = gfin.at[q, m, : HALF - QUARTER, :]
        remote(others, others, s4.at[q, m], r4.at[q, m], to_y).wait()
        c4_here(q, m).wait()
        c5(q, m).start()

    def each(stage, which=(0, 1, 2)):
        def run(q):
            for m in which:
                stage(q, m)

        run.__name__ = stage.__name__
        return run

    def when(test, what, q):
        def run():
            with jax.named_scope(what.__name__):
                what(q)
        pl.when(test)(run)

    last = 2 * CHUNKS

    def exchange(q, b):
        def at(stage, back, what, which=(0, 1, 2)):
            when((b == stage) & (q >= back), each(what, which), q - back)

        at(0, 2, g2, (2,))
        at(0, 1, g0)
        at(0, 3, g4, (2,))
        at(1, 1, g1)
        at(1, 2, g3, (0, 1))
        at(1, 3, g5, (0, 1))
        at(2, 2, g3, (2,))
        at(2, 3, g5, (2,))
        at(3, 1, g2, (0, 1))
        at(3, 2, g4, (0, 1))

    def drain():
        a, b, c = last - 3, last - 2, last - 1
        each(g0)(c)
        g2(b, 2)
        g4(a, 2)
        each(g3, (0, 1))(b)
        each(g1)(c)
        each(g5, (0, 1))(a)
        g3(b, 2)
        each(g4, (0, 1))(b)
        g5(a, 2)
        g2(c, 0)
        g4(b, 2)
        g2(c, 1)
        g3(c, 0)
        each(g5, (0, 1))(b)
        g2(c, 2)
        g3(c, 1)
        g5(b, 2)
        g4(c, 0)
        g3(c, 2)
        g4(c, 1)
        g5(c, 0)
        g4(c, 2)
        over_r[me_r] = squares[...]
        peers_r = [to_peer(k) for k in range(YS * ZS - 1)]
        from_r = [lax.rem(me_r + YS * ZS - 1 - k, YS * ZS) for k in range(YS * ZS - 1)]
        peers_s = [{"r": me_r, "s": lax.rem(me_s + 1 + k, OWNERS)} for k in range(OWNERS - 1)]
        from_s = [lax.rem(me_s + OWNERS - 1 - k, OWNERS) for k in range(OWNERS - 1)]
        tell(me_r, over_r, sn, rn, peers_r)
        g5(c, 1)
        hear(me_r, over_r, sn, rn, peers_r, from_r)
        over_s[me_s] = jnp.sum(over_r[...], 0)
        tell(me_s, over_s, sm, rm, peers_s)
        g5(c, 2)
        hear(me_s, over_s, sm, rm, peers_s, from_s)

    def tell(me, scratch, send, recv, others):
        for k, where in enumerate(others):
            remote(scratch.at[me], scratch.at[me], send.at[k], recv.at[k], where).start()

    def hear(me, scratch, send, recv, others, places):
        for k, (where, place) in enumerate(zip(others, places)):
            remote(scratch.at[me], scratch.at[place], send.at[k], recv.at[k], where).wait()

    def normed(wide):
        scale = lax.rsqrt(jnp.mean(wide * wide, -1, keepdims=True) + 1e-6)
        return (wide * scale).astype(bf16)

    def tile(t, n=Tt):
        return pl.ds(pl.multiple_of(t * n, n), n)

    def first(wslot, t, slot, backward, r, c):
        s = pl.ds(pl.multiple_of(t * Tt + r * rb, rb), rb)
        rs, cs = slice(r * rb, (r + 1) * rb), slice(c * cb, (c + 1) * cb)
        a = A[s, :]
        g = dotn(a, W[wslot, 0, :, cs])
        u = dotn(a, W[wslot, 1, :, cs])
        h = 0.5 * g
        th = jnp.tanh(h)
        silu = h * th + h
        if not backward:
            act_s[slot, rs, cs] = (silu * u).astype(bf16)
            return
        d = dott(DH[s, :], W[wslot, 2, cs, :]).astype(bf16).astype(f32)
        sig = 0.5 * th + 0.5
        act_s[slot, rs, cs] = (silu * u).astype(bf16)
        du_s[slot, rs, cs] = (d * silu).astype(bf16)
        dg_s[slot, rs, cs] = (d * u * (sig * (1.0 + g - silu))).astype(bf16)

    def second(wslot, t, slot, backward, input_too, begin, which):
        s = tile(t)
        if not backward:
            total[s, :] += dotn(act_s[slot], W[wslot, 2])
            return
        if which == 3:
            total[s, :] += dott(dg_s[slot], W[wslot, 0]) + dott(du_s[slot], W[wslot, 1])
            return
        if which == 2:
            new = dot0(act_s[slot], DH[s, :])
        else:
            new = dot0(A[s, :], (dg_s, du_s)[which][slot])
        if begin:
            accs[which] = jnp.where(t == 0, 0.0, accs[which]) + new
        else:
            accs[which] += new

    blocks = [(r, c) for r in range(Tt // rb) for c in range(F // cb)]

    def together(w1, t1, slot1, w2, t2, slot2, backward, input_too, begin):
        for which in range(4 if input_too else 3) if backward else [0]:
            second(w2, t2, slot2, backward, input_too, begin, which)
        for block in blocks:
            first(w1, t1, slot1, backward, *block)

    def phase(base, backward, input_too):
        for block in blocks:
            first(lax.rem(base, 2), 0, 0, backward, *block)

        def step(i, _):
            n, b = base + i // per, lax.rem(i, per)
            if backward:
                exchange(n - CHUNKS, b)
            if base < 2 * CHUNKS:
                when((b == 0) & (n + 4 < 2 * CHUNKS), send_own, n + 4)
                when((b == 1) & (n + 1 < 2 * CHUNKS), forward, n + 1)
            when((b == 2) & (n + 1 < 3 * CHUNKS), load, n + 1)
            when((b == per - 1) & (n + 1 < 3 * CHUNKS), wait_load, n + 1)
            w = lax.rem(n, 2)
            t = 2 * b
            together(w, t + 1, 1, w, t, 0, backward, input_too, True)
            over = b == per - 1
            together(jnp.where(over, 1 - w, w), jnp.where(over, 0, t + 2), 0, w, t + 1, 1, backward, input_too, False)
            return 0

        lax.fori_loop(0, per * CHUNKS, step, 0)

    barrier = pltpu.get_barrier_semaphore()
    peers = [to_partner, to_across] + [{"r": lax.rem(me_r + k, YS * ZS), "s": me_s} for k in range(1, YS * ZS)]
    for peer in peers:
        pl.semaphore_signal(barrier, inc=1, device_id=peer, device_id_type=MESH)
    load_x = pltpu.make_async_copy(x_hbm, H, in_sem.at[0])
    load_dy = pltpu.make_async_copy(dy_hbm, DH, in_sem.at[1])
    load_x.start()
    load_dy.start()
    with jax.named_scope('barrier'):
        pl.semaphore_wait(barrier, len(peers))
    lax.fori_loop(0, 4, lambda c, _: (send_own(c), 0)[1], 0)
    load_x.wait()

    def begin(t, _):
        s = tile(t, rb)
        A[s, :] = normed(H[s, :].astype(f32))
        total[s, :] = jnp.zeros((rb, D), f32)
        return 0

    squares[...] = jnp.zeros(squares.shape, f32)
    with jax.named_scope('begin'):
        lax.fori_loop(0, T // rb, begin, 0)
    save_a = pltpu.make_async_copy(A, a0_hbm, in_sem.at[0])
    save_a.start()
    with jax.named_scope('first_load'):
        forward(0)
        load(0)
        wait_load(0)
    with jax.named_scope('p_fwd'):
        phase(0, False, False)
    save_a.wait()
    load_dy.wait()

    def between(t, _):
        s = tile(t, rb)
        h = (H[s, :].astype(f32) + total[s, :].astype(bf16).astype(f32)).astype(bf16)
        H[s, :] = h
        A[s, :] = normed(h.astype(f32))
        total[s, :] = jnp.zeros((rb, D), f32)
        return 0

    with jax.named_scope('between'):
        lax.fori_loop(0, T // rb, between, 0)
    with jax.named_scope('p_one'):
        phase(CHUNKS, True, True)
    load_a = pltpu.make_async_copy(a0_hbm, A, in_sem.at[0])
    load_a.start()

    def back(t, _):
        s = tile(t, rb)
        wide = H[s, :].astype(f32)
        da = total[s, :].astype(bf16).astype(f32)
        scale = lax.rsqrt(jnp.mean(wide * wide, -1, keepdims=True) + 1e-6)
        along = jnp.sum(da * wide, -1, keepdims=True) * (scale * scale * scale * (1.0 / D))
        dn = (da * scale - wide * along).astype(bf16).astype(f32)
        DH[s, :] = (DH[s, :].astype(f32) + dn).astype(bf16)
        return 0

    with jax.named_scope('back'):
        lax.fori_loop(0, T // rb, back, 0)
        load_a.wait()
    fetch = [pltpu.make_async_copy(src, dst, early_sem.at[i]) for i, (src, dst) in enumerate(zip(early, early_out))]
    for copy in fetch:
        copy.start()
    with jax.named_scope('p_zero'):
        phase(2 * CHUNKS, True, False)

    with jax.named_scope("drain"):
        drain()
    with jax.named_scope("norm"):
        mean = jnp.sum(over_s[...]) * (1.0 / COUNT)
        factor[...] = jnp.minimum(1.0, 0.5 * lax.rsqrt(jnp.full(factor.shape, mean + 1e-30, f32)))

    def finish(q, _):
        for m in range(3):
            c5(q, m).wait()
        l, j = q // CHUNKS, lax.rem(q, CHUNKS)
        two = wbuf.at[l, j, :, : R, :]
        for k in range(2):
            remote(two, two, ws_send.at[k, q], w_recv.at[0, q], to_partner).wait_send()
        remote(two, two, wf_send.at[q], w_recv.at[0, q], to_partner).wait_send()
        return 0

    for copy in fetch:
        copy.wait()
    with jax.named_scope('finish'):
        lax.fori_loop(0, last, finish, 0)


def gradients_of(x, dy, w_gate, w_up, w_down, early, tiles=(512, 256, 256), vmem=41 * 2**20):
    T, D = x.shape
    F = w_gate.shape[2] // CHUNKS
    Tt, rb, cb = tiles
    R = D // OWNERS
    H, Q = R // YS, R // (YS * ZS)
    n = 2 * CHUNKS
    lanes = min(F, 128)
    vm = pltpu.VMEM
    dma, hbm = pltpu.SemaphoreType.DMA, pl.BlockSpec(memory_space=pltpu.HBM)
    outs = pl.pallas_call(
        functools.partial(kernel, (T, D, F, Tt, rb, cb, lanes)),
        in_specs=[hbm] * (5 + len(early)),
        out_specs=[hbm, pl.BlockSpec(memory_space=pltpu.VMEM), hbm, hbm] + [pl.BlockSpec(memory_space=pltpu.VMEM)] * len(early),
        out_shape=[
            pltpu.HBM((n, 3, R, F), bf16), pltpu.VMEM((8, 128), f32),
            pltpu.HBM((2, CHUNKS, 3, D, F), bf16), pltpu.HBM((T, D), bf16),
            *(pltpu.VMEM(a.shape, a.dtype) for a in early),
        ],
        scratch_shapes=[
            vm((T, D), bf16), vm((T, D), bf16), vm((T, D), bf16), vm((T, D), f32),
            vm((2, 3, D, F), bf16), vm((2, Tt, F), bf16), vm((2, Tt, F), bf16), vm((2, Tt, F), bf16), vm((3, D, F), f32),
            vm((3, XS, R, F), bf16), vm((2, 3, XS, R, F), bf16), vm((3, XS, R, F), f32),
            vm((3, R, F), bf16), vm((2, 3, R, F), bf16), vm((3, R, F), f32),
            vm((3, H, F), bf16), vm((2, 3, H, F), bf16), vm((3, H, F), f32),
            vm((3, ZS - 1, Q, F), bf16), vm((2, 3, ZS - 1, Q, F), bf16), vm((3, Q, F), f32),
            vm((n, 3, Q, F), bf16), vm((Q, lanes), f32), vm((YS * ZS, Q, lanes), f32), vm((OWNERS, Q, lanes), f32),
            dma((2,)), dma((len(early),)), dma((2,)), dma((n, 3)),
            dma((2, n)), dma((n,)), dma((3, n)),
            dma((3,)), dma((2, 3)), dma((3,)), dma((2, 3)), dma((3,)), dma((2, 3)), dma((3, ZS - 1)), dma((2, 3, ZS - 1)), dma((n, 3)), dma((n, 3)), dma((n, 3)), dma((n, 3)),
            dma((YS * ZS - 1,)), dma((YS * ZS - 1,)), dma((OWNERS - 1,)), dma((OWNERS - 1,)),
        ],
        compiler_params=pltpu.CompilerParams(collective_id=0, has_side_effects=True, vmem_limit_bytes=vmem),
    )(*(pltpu.with_memory_space_constraint(a, pltpu.HBM) for a in (x, dy, w_gate, w_up, w_down, *early)))
    return outs[0], outs[1], outs[4:]


def update(factor, ga, gb, gc, *refs):
    l, o = pl.program_id(0), pl.program_id(1)
    scale = factor[0:1, 0:1]
    for i, g in enumerate((ga, gb, gc)):
        _, parts, _, R, wide = g.shape
        size = wide if i < 2 else R
        for j in range(parts):
            near = slice(j * size, (j + 1) * size)
            far = pl.ds(pl.multiple_of((o * parts + j) * size, size), size)

            def read(kind):
                ref, layer, cut = (refs[3 * kind + i], l, far) if (kind, i) in EARLY else (refs[3 * kind + i], 0, near)
                return ref[layer, :, cut] if i < 2 else ref[layer, cut, :]

            def write(kind, value):
                if i < 2:
                    refs[9 + 3 * kind + i][0, :, near] = value
                else:
                    refs[9 + 3 * kind + i][0, near, :] = value

            gradient = g[0, j, 0].astype(f32) * scale
            m = 0.9 * read(1) + 0.1 * gradient
            v = 0.95 * read(2) + 0.05 * gradient * gradient
            w = read(0).astype(f32)
            write(0, (w - 0.02 * (m * lax.rsqrt(v + 1e-8) + 0.1 * w)).astype(bf16))
            write(1, m)
            write(2, v)


def updated(g, factor, weights, m, v):
    _, _, _, R, F = g.shape
    wide = F // OWNERS
    at = pl.BlockSpec
    native = [at((1, R, CHUNKS * wide), lambda l, o: (l, 0, o))] * 2 + [at((1, CHUNKS * R // OWNERS, F), lambda l, o: (l, o, 0))]
    mine = [at((1, CHUNKS, 1, R, wide), lambda l, o, k=k: (1 - l, 0, k, 0, o)) for k in range(2)]
    mine.append(at((1, CHUNKS // OWNERS, 1, R, F), lambda l, o: (1 - l, o, 2, 0, 0)))
    arrays, specs = [], []
    for kind, three in enumerate((weights, m, v)):
        for i, a in enumerate(three):
            early = (kind, i) in EARLY
            arrays.append(pltpu.with_memory_space_constraint(a, pltpu.VMEM if early else pltpu.HBM))
            specs.append(at(memory_space=pltpu.VMEM) if early else native[i])
    g = pltpu.with_memory_space_constraint(g, pltpu.HBM)
    return pl.pallas_call(
        update,
        grid=(2, OWNERS),
        in_specs=[at((8, 128), lambda l, o: (0, 0)), *mine, *specs],
        out_specs=native * 3,
        out_shape=[jax.ShapeDtypeStruct(a.shape, a.dtype) for a in arrays],
        compiler_params=pltpu.CompilerParams(vmem_limit_bytes=15 * 2**20),
    )(factor, g, g, g, *arrays)


def solution(mesh, **options):
    def step(x, dy, *arrays):
        weights, m, v = (arrays[i : i + 3] for i in (0, 3, 6))
        state = [weights, m, v]
        g, factor, early = gradients_of(x[0], dy[0], *weights, [state[kind][i] for kind, i in EARLY], **options)
        state = [list(three) for three in state]
        for (kind, i), a in zip(EARLY, early):
            state[kind][i] = a
        return tuple(updated(g.reshape(2, CHUNKS, *g.shape[1:]), factor, *state))

    states, cut = P(("rep", "r", "s"), None, None), P(None, "s", None)
    return jax.shard_map(
        step,
        mesh=mesh,
        in_specs=(states, states) + (cut,) * 9,
        out_specs=(P("rep", "s", None),) * 9,
        check_vma=False,
    )
```

time: 477 us -> 444 us (0.931)
  other arithmetic: 33.7 us -> 0 us
  Pallas kernels: 434 us -> 443 us
  blocking collectives: 6.27 us -> 0 us
    convert_element_type x2 -> x0, other arithmetic: 23.7 us -> none  [adamw(): return ((w - 0.02 * step).astype(bf16), m, v)]
    reduce_sum x3 -> x0, other arithmetic: 9.97 us -> none  [step(): squares = lax.psum(sum((jnp.sum(g * g) for g in gradients)), 's')]
    pallas_call x1 -> x2, Pallas kernels: 434 us -> 443 us  [the longest x1 424 us: gradients_of(): pl.pallas_call(functools.partial(kernel, (T, D, F, Tt, rb, cb, lanes)), i...]
    psum x1 -> x0, blocking collectives: 6.27 us -> none  [step(): squares = lax.psum(sum((jnp.sum(g * g) for g in gradients)), 's')]
where the time goes in v2:
time: 444 us
  Pallas kernels  443 us (100%)
    pallas_call x1, Pallas kernels, gradients_of(): pl.pallas_call(functools.partial(kernel, (T, D, F, Tt, rb, cb, lanes)), i...  424 us
    pallas_call x1, Pallas kernels, updated(): pl.pallas_call(update, grid=(2, OWNERS), in_specs=[at((8, 128), lambda l,...  19.2 us

profile of v2, /device:TPU:0, one launch (start us, length us, event | category | flops | bytes accessed | tf_op | source)
XLA Modules:
  0.0 443.8 jit_solution(10889674403460774463)
XLA Ops:
  0.6 423.8 %shard_map.178 = (bf16[16,3,128,512]{3,2,1,0:T(8,128)(2,1)}, f32[8,128]{1,0:T(8,128)S(1)}, bf16[2,8,3,512,512]{4,3,2,1,0:T(8,128)(2,1)}, bf16[4096,512]{1,0:T(8,...) custom-call(bf16[4096,512]{1,0:T(8,128)(2,1)} %bitcast.6, ...), custom_call_target="tpu_custom_call" | custom-call | tf_op jit(solution)/shard_map/pallas_call | solution.py:449
  424.5 19.2 %shard_map.179 = (bf16[2,128,4096]{2,1,0:T(8,128)(2,1)}, bf16[2,128,4096]{2,1,0:T(8,128)(2,1)}, bf16[2,1024,512]{2,1,0:T(8,128)(2,1)}, f32[2,128,4096]{2,1,0:T(8...) custom-call(f32[8,128]{1,0:T(8,128)S(1)} %get-tuple-element.16.facto, ...), custom_call_target="tpu_custom_call" | custom-call | tf_op jit(solution)/shard_map/pallas_call | solution.py:519

commit v3 on v2

--- a/solution.py
+++ b/solution.py
@@ -9,6 +9,7 @@
 
 MESH = pl.DeviceIdType.MESH
 CHUNKS, CORES, XS, YS, ZS, OWNERS = 8, 2, 2, 2, 4, 4
+FIRST = 0
 f32, bf16 = jnp.float32, jnp.bfloat16
 
 EARLY = ((1, 0), (1, 1), (1, 2), (2, 0), (2, 1))
@@ -64,41 +65,65 @@
     def rows(owner):
         return pl.ds(pl.multiple_of(owner * R, R), R)
 
-    def own_pieces(l, j, into):
+    def half(h):
+        return pl.ds(pl.multiple_of(h * HALF, HALF), HALF)
+
+    def part_of(owner, h):
+        return pl.ds(pl.multiple_of(owner * R + h * HALF, HALF), HALF)
+
+    def own_pieces(l, j, into, h=None):
         wide = F // OWNERS
+        there = rows(me_s) if h is None else part_of(me_s, h)
         for m, w in ((0, wg_hbm), (1, wu_hbm)):
             for o in range(OWNERS):
                 cols = pl.ds(pl.multiple_of(o * wide * CHUNKS + j * wide, wide), wide)
-                yield w.at[l, :, cols], into.at[m, rows(me_s), o * wide : (o + 1) * wide]
-        yield wd_hbm.at[l, rows(j), :], into.at[2, rows(me_s), :]
+                src = w.at[l, :, cols] if h is None else w.at[l, half(h), cols]
+                yield m, src, into.at[m, there, o * wide : (o + 1) * wide]
+        here = rows(j) if h is None else part_of(j, h)
+        yield 2, wd_hbm.at[l, here, :], into.at[2, there, :]
+
+    def chunk_of(c):
+        return c // CHUNKS, lax.rem(c, CHUNKS)
 
     def send_own(c):
-        l, j = c // CHUNKS, lax.rem(c, CHUNKS)
-        for src, dst in own_pieces(l, j, wbuf.at[l, j]):
-            remote(src, dst, ws_send.at[0, c], w_recv.at[0, c], to_across).start()
-        for src, dst in own_pieces(l, j, wbuf.at[l, j]):
-            remote(src, dst, ws_send.at[1, c], w_recv.at[1, c], to_partner).start()
-
-    def package(c, owner):
-        return wbuf.at[c // CHUNKS, lax.rem(c, CHUNKS), :, rows(owner), :]
-
-    def wait_package(kind, c, owner):
-        remote(package(c, owner), package(c, owner), wf_send.at[c], w_recv.at[kind, c], to_partner).wait_recv()
-
-    def forward(c):
-        wait_package(0, c, across)
-        remote(package(c, across), package(c, across), wf_send.at[c], w_recv.at[2, c], to_partner).start()
+        l, j = chunk_of(c)
+        for m, src, dst in own_pieces(l, j, wbuf.at[l, j], my):
+            at = m if c is FIRST else c + 2
+            remote(src, dst, ws_send.at[0, c], w_recv.at[0, at], to_across).start()
+        for m, src, dst in own_pieces(l, j, wbuf.at[l, j]):
+            remote(src, dst, ws_send.at[1, c], w_recv.at[1, c + 2], to_partner).start()
+
+    def pass_on(kind, c, owner, h, where, m=None):
+        l, j = chunk_of(c)
+        part = wbuf.at[l, j, :, part_of(owner, h), :] if m is None else wbuf.at[l, j, m, part_of(owner, h), :]
+        at = c + 2 if m is None else m
+        return remote(part, part, wf_send.at[max(kind - 2, 0), at], w_recv.at[kind, at], where)
+
+    def forward(c, m=None):
+        pass_on(0, c, across, my, to_across, m).wait_recv()
+        pass_on(3, c, across, my, to_y, m).start()
+        pass_on(2, c, across, my, to_partner, m).start()
+
+    def forward2(c, m=None):
+        pass_on(3, c, across, 1 - my, to_y, m).wait_recv()
+        pass_on(4, c, across, 1 - my, to_partner, m).start()
 
     def load(n):
         slot = lax.rem(n, 2)
         l, j = lax.rem(n // CHUNKS, 2), lax.rem(n, CHUNKS)
 
-        @pl.when(n < 2 * CHUNKS)
-        def _():
-            wait_package(1, n, partner)
-            wait_package(2, n, (1 - mx) * CORES + 1 - core)
-
-        for src, dst in own_pieces(l, j, W.at[slot]):
+        def wait_all(each):
+            whole = wbuf.at[l, j, :, rows(partner), :]
+            remote(whole, whole, ws_send.at[1, n], w_recv.at[1, n + 2], to_partner).wait_recv()
+            for m in each:
+                pass_on(2, n, partner, my, to_partner, m).wait_recv()
+                pass_on(4, n, partner, 1 - my, to_partner, m).wait_recv()
+
+        if n is FIRST:
+            wait_all(range(3))
+        else:
+            pl.when(n < 2 * CHUNKS)(lambda: wait_all([None]))
+        for _, src, dst in own_pieces(l, j, W.at[slot]):
             pltpu.make_async_copy(src, dst, w_sem.at[slot]).start()
         for k in range(1, OWNERS):
             o = lax.rem(me_s + k, OWNERS)
@@ -130,9 +155,6 @@
         own1[m] = own0[m, mx] + rb0[slot, m, mx].astype(f32)
         c1(q, m).start()
 
-    def half(h):
-        return pl.ds(pl.multiple_of(h * HALF, HALF), HALF)
-
     def c2(q, m):
         slot = lax.rem(q, 2)
         return remote(sb2.at[m], rb2.at[slot, m], s2.at[m], r2.at[slot, m], to_y)
@@ -169,10 +191,10 @@
 
     def c4(q, m, k):
         where = {"r": my * ZS + lax.rem(mz + 1 + k, ZS), "s": me_s}
-        return remote(piece.at[q, m], gfin.at[q, m, mine, :], s4.at[q, m], r4.at[q, m], where)
+        return remote(piece.at[q, m], gfin.at[q, m, mine, :], s4.at[lax.rem(q, 2), m], r4.at[lax.rem(q, 2), m], where)
 
     def c4_here(q, m):
-        return pltpu.make_async_copy(piece.at[q, m], gfin.at[q, m, mine, :], out_sem.at[q, m])
+        return pltpu.make_async_copy(piece.at[q, m], gfin.at[q, m, mine, :], out_sem.at[lax.rem(q, 2), m])
 
     def g4(q, m):
         slot = lax.rem(q, 2)
@@ -191,13 +213,16 @@
 
     def c5(q, m):
         part = gfin.at[q, m, half(my), :]
-        return remote(part, part, s5.at[q, m], r5.at[q, m], to_y)
+        return remote(part, part, s5.at[lax.rem(q, 2), m], r5.at[lax.rem(q, 2), m], to_y)
 
     def g5(q, m):
         others = gfin.at[q, m, : HALF - QUARTER, :]
-        remote(others, others, s4.at[q, m], r4.at[q, m], to_y).wait()
+        remote(others, others, s4.at[lax.rem(q, 2), m], r4.at[lax.rem(q, 2), m], to_y).wait()
         c4_here(q, m).wait()
         c5(q, m).start()
+
+    def g6(q, m):
+        c5(q, m).wait()
 
     def each(stage, which=(0, 1, 2)):
         def run(q):
@@ -216,24 +241,23 @@
     last = 2 * CHUNKS
 
     def exchange(q, b):
-        def at(stage, back, what, which=(0, 1, 2)):
-            when((b == stage) & (q >= back), each(what, which), q - back)
-
-        at(0, 2, g2, (2,))
-        at(0, 1, g0)
-        at(0, 3, g4, (2,))
-        at(1, 1, g1)
-        at(1, 2, g3, (0, 1))
-        at(1, 3, g5, (0, 1))
-        at(2, 2, g3, (2,))
-        at(2, 3, g5, (2,))
-        at(3, 1, g2, (0, 1))
-        at(3, 2, g4, (0, 1))
+        def at(stage, *parts):
+            @pl.when(b == stage)
+            def _():
+                for back, what, which in parts:
+                    when(q >= back, each(what, which), q - back)
+
+        every = (0, 1, 2)
+        at(0, (2, g2, (2,)), (1, g0, every), (3, g4, (2,)), (4, g6, every))
+        at(1, (1, g1, every), (2, g3, (0, 1)), (3, g5, (0, 1)))
+        at(2, (2, g3, (2,)), (3, g5, (2,)))
+        at(3, (1, g2, (0, 1)), (2, g4, (0, 1)))
 
     def drain():
         a, b, c = last - 3, last - 2, last - 1
         each(g0)(c)
         g2(b, 2)
+        each(g6)(a - 1)
         g4(a, 2)
         each(g3, (0, 1))(b)
         each(g1)(c)
@@ -243,6 +267,7 @@
         g5(a, 2)
         g2(c, 0)
         g4(b, 2)
+        each(g6)(a)
         g2(c, 1)
         g3(c, 0)
         each(g5, (0, 1))(b)
@@ -252,6 +277,7 @@
         g4(c, 0)
         g3(c, 2)
         g4(c, 1)
+        each(g6)(b)
         g5(c, 0)
         g4(c, 2)
         over_r[me_r] = squares[...]
@@ -266,6 +292,7 @@
         tell(me_s, over_s, sm, rm, peers_s)
         g5(c, 2)
         hear(me_s, over_s, sm, rm, peers_s, from_s)
+        each(g6)(c)
 
     def tell(me, scratch, send, recv, others):
         for k, where in enumerate(others):
@@ -334,8 +361,16 @@
             if backward:
                 exchange(n - CHUNKS, b)
             if base < 2 * CHUNKS:
-                when((b == 0) & (n + 4 < 2 * CHUNKS), send_own, n + 4)
-                when((b == 1) & (n + 1 < 2 * CHUNKS), forward, n + 1)
+
+                @pl.when(b == 0)
+                def _():
+                    when(n + 4 < 2 * CHUNKS, send_own, n + 4)
+
+                @pl.when(b == 1)
+                def _():
+                    when(n + 1 < 2 * CHUNKS, forward2, n + 1)
+                    when(n + 2 < 2 * CHUNKS, forward, n + 2)
+
             when((b == 2) & (n + 1 < 3 * CHUNKS), load, n + 1)
             when((b == per - 1) & (n + 1 < 3 * CHUNKS), wait_load, n + 1)
             w = lax.rem(n, 2)
@@ -357,7 +392,8 @@
     load_dy.start()
     with jax.named_scope('barrier'):
         pl.semaphore_wait(barrier, len(peers))
-    lax.fori_loop(0, 4, lambda c, _: (send_own(c), 0)[1], 0)
+    send_own(FIRST)
+    lax.fori_loop(1, 4, lambda c, _: (send_own(c), 0)[1], 0)
     load_x.wait()
 
     def begin(t, _):
@@ -372,8 +408,12 @@
     save_a = pltpu.make_async_copy(A, a0_hbm, in_sem.at[0])
     save_a.start()
     with jax.named_scope('first_load'):
-        forward(0)
-        load(0)
+        for m in range(3):
+            forward(FIRST, m)
+        for m in range(3):
+            forward2(FIRST, m)
+        load(FIRST)
+        forward(1)
         wait_load(0)
     with jax.named_scope('p_fwd'):
         phase(0, False, False)
@@ -421,13 +461,19 @@
         factor[...] = jnp.minimum(1.0, 0.5 * lax.rsqrt(jnp.full(factor.shape, mean + 1e-30, f32)))
 
     def finish(q, _):
-        for m in range(3):
-            c5(q, m).wait()
         l, j = q // CHUNKS, lax.rem(q, CHUNKS)
-        two = wbuf.at[l, j, :, : R, :]
-        for k in range(2):
-            remote(two, two, ws_send.at[k, q], w_recv.at[0, q], to_partner).wait_send()
-        remote(two, two, wf_send.at[q], w_recv.at[0, q], to_partner).wait_send()
+        one = wbuf.at[l, j, :, :R, :]
+        remote(one, one, ws_send.at[1, q], w_recv.at[1, q + 2], to_partner).wait_send()
+        one = wbuf.at[l, j, :, :HALF, :]
+        remote(one, one, ws_send.at[0, q], w_recv.at[0, q + 2], to_across).wait_send()
+
+        def passed(each):
+            for m in each:
+                for kind in (2, 3, 4):
+                    pass_on(kind, q, across, my, to_partner, m).wait_send()
+
+        pl.when(q == 0)(lambda: passed(range(3)))
+        pl.when(q > 0)(lambda: passed([None]))
         return 0
 
     for copy in fetch:
@@ -463,9 +509,9 @@
             vm((3, H, F), bf16), vm((2, 3, H, F), bf16), vm((3, H, F), f32),
             vm((3, ZS - 1, Q, F), bf16), vm((2, 3, ZS - 1, Q, F), bf16), vm((3, Q, F), f32),
             vm((n, 3, Q, F), bf16), vm((Q, lanes), f32), vm((YS * ZS, Q, lanes), f32), vm((OWNERS, Q, lanes), f32),
-            dma((2,)), dma((len(early),)), dma((2,)), dma((n, 3)),
-            dma((2, n)), dma((n,)), dma((3, n)),
-            dma((3,)), dma((2, 3)), dma((3,)), dma((2, 3)), dma((3,)), dma((2, 3)), dma((3, ZS - 1)), dma((2, 3, ZS - 1)), dma((n, 3)), dma((n, 3)), dma((n, 3)), dma((n, 3)),
+            dma((2,)), dma((len(early),)), dma((2,)), dma((2, 3)),
+            dma((2, n)), dma((3, n + 2)), dma((5, n + 2)),
+            dma((3,)), dma((2, 3)), dma((3,)), dma((2, 3)), dma((3,)), dma((2, 3)), dma((3, ZS - 1)), dma((2, 3, ZS - 1)), dma((2, 3)), dma((2, 3)), dma((2, 3)), dma((2, 3)),
             dma((YS * ZS - 1,)), dma((YS * ZS - 1,)), dma((OWNERS - 1,)), dma((OWNERS - 1,)),
         ],
         compiler_params=pltpu.CompilerParams(collective_id=0, has_side_effects=True, vmem_limit_bytes=vmem),

time: 444 us -> 431 us (0.971)
  Pallas kernels: 443 us -> 430 us
    pallas_call x1, Pallas kernels: 424 us -> 411 us  [gradients_of(): pl.pallas_call(functools.partial(kernel, (T, D, F, Tt, rb, cb, lanes)), i...]
where the time goes in v3:
time: 431 us
  Pallas kernels  430 us (100%)
    pallas_call x1, Pallas kernels, gradients_of(): pl.pallas_call(functools.partial(kernel, (T, D, F, Tt, rb, cb, lanes)), i...  411 us
    pallas_call x1, Pallas kernels, updated(): pl.pallas_call(update, grid=(2, OWNERS), in_specs=[at((8, 128), lambda l,...  19.2 us

profile of v3, /device:TPU:0, one launch (start us, length us, event | category | flops | bytes accessed | tf_op | source)
XLA Modules:
  0.0 431.2 jit_solution(12164989602365547328)
XLA Ops:
  0.6 411.2 %shard_map.178 = (bf16[16,3,128,512]{3,2,1,0:T(8,128)(2,1)}, f32[8,128]{1,0:T(8,128)S(1)}, bf16[2,8,3,512,512]{4,3,2,1,0:T(8,128)(2,1)}, bf16[4096,512]{1,0:T(8,...) custom-call(bf16[4096,512]{1,0:T(8,128)(2,1)} %bitcast.6, ...), custom_call_target="tpu_custom_call" | custom-call | tf_op jit(solution)/shard_map/pallas_call | solution.py:495
  411.8 19.2 %shard_map.179 = (bf16[2,128,4096]{2,1,0:T(8,128)(2,1)}, bf16[2,128,4096]{2,1,0:T(8,128)(2,1)}, bf16[2,1024,512]{2,1,0:T(8,128)(2,1)}, f32[2,128,4096]{2,1,0:T(8...) custom-call(f32[8,128]{1,0:T(8,128)S(1)} %get-tuple-element.16.facto, ...), custom_call_target="tpu_custom_call" | custom-call | tf_op jit(solution)/shard_map/pallas_call | solution.py:565

commit v4 on v3

--- a/solution.py
+++ b/solution.py
@@ -12,9 +12,6 @@
 FIRST = 0
 f32, bf16 = jnp.float32, jnp.bfloat16
 
-EARLY = ((1, 0), (1, 1), (1, 2), (2, 0), (2, 1))
-
-
 def dotn(a, b):
     return jnp.dot(a, b, preferred_element_type=f32)
 
@@ -31,16 +28,16 @@
     sizes,
     x_hbm, dy_hbm, wg_hbm, wu_hbm, wd_hbm, *refs,
 ):
-    early, refs = refs[: len(EARLY)], refs[len(EARLY) :]
-    kernel_(sizes, x_hbm, dy_hbm, wg_hbm, wu_hbm, wd_hbm, early, refs[4 : 4 + len(EARLY)], *refs[:4], *refs[4 + len(EARLY) :])
+    early, refs = refs[:5], refs[5:]
+    kernel_(sizes, x_hbm, dy_hbm, wg_hbm, wu_hbm, wd_hbm, early, refs[4:9], *refs[:4], *refs[9:])
 
 
 def kernel_(
     sizes,
     x_hbm, dy_hbm, wg_hbm, wu_hbm, wd_hbm, early, early_out, gfin, factor, wbuf, a0_hbm,
-    A, DH, H, total, W, act_s, du_s, dg_s, accs,
+    H, A, DH, total, W, act_s, du_s, dg_s, accs,
     sb0, rb0, own0, sb1, rb1, own1, sb2, rb2, own2, sb3, rb3, own3, piece, squares, over_r, over_s,
-    in_sem, early_sem, w_sem, out_sem,
+    in_sem, early_sem, w_sem, keep_sem, out_sem,
     ws_send, wf_send, w_recv,
     s0, r0, s1, r1, s2, r2, s3, r3, s4, r4, s5, r5, sn, rn, sm, rm,
 ):
@@ -87,15 +84,16 @@
 
     def send_own(c):
         l, j = chunk_of(c)
-        for m, src, dst in own_pieces(l, j, wbuf.at[l, j], my):
+        into = W.at[0] if c is FIRST else wbuf.at[l, j]
+        for m, src, dst in own_pieces(l, j, into, my):
             at = m if c is FIRST else c + 2
             remote(src, dst, ws_send.at[0, c], w_recv.at[0, at], to_across).start()
-        for m, src, dst in own_pieces(l, j, wbuf.at[l, j]):
+        for m, src, dst in own_pieces(l, j, into):
             remote(src, dst, ws_send.at[1, c], w_recv.at[1, c + 2], to_partner).start()
 
     def pass_on(kind, c, owner, h, where, m=None):
         l, j = chunk_of(c)
-        part = wbuf.at[l, j, :, part_of(owner, h), :] if m is None else wbuf.at[l, j, m, part_of(owner, h), :]
+        part = wbuf.at[l, j, :, part_of(owner, h), :] if m is None else W.at[0, m, part_of(owner, h), :]
         at = c + 2 if m is None else m
         return remote(part, part, wf_send.at[max(kind - 2, 0), at], w_recv.at[kind, at], where)
 
@@ -112,22 +110,40 @@
         slot = lax.rem(n, 2)
         l, j = lax.rem(n // CHUNKS, 2), lax.rem(n, CHUNKS)
 
-        def wait_all(each):
+        @pl.when(n < 2 * CHUNKS)
+        def _():
             whole = wbuf.at[l, j, :, rows(partner), :]
             remote(whole, whole, ws_send.at[1, n], w_recv.at[1, n + 2], to_partner).wait_recv()
-            for m in each:
-                pass_on(2, n, partner, my, to_partner, m).wait_recv()
-                pass_on(4, n, partner, 1 - my, to_partner, m).wait_recv()
-
-        if n is FIRST:
-            wait_all(range(3))
-        else:
-            pl.when(n < 2 * CHUNKS)(lambda: wait_all([None]))
+            pass_on(2, n, partner, my, to_partner).wait_recv()
+            pass_on(4, n, partner, 1 - my, to_partner).wait_recv()
+
         for _, src, dst in own_pieces(l, j, W.at[slot]):
             pltpu.make_async_copy(src, dst, w_sem.at[slot]).start()
         for k in range(1, OWNERS):
             o = lax.rem(me_s + k, OWNERS)
             pltpu.make_async_copy(wbuf.at[l, j, :, rows(o), :], W.at[slot, :, rows(o), :], w_sem.at[slot]).start()
+
+    def load_first():
+        for _, src, dst in own_pieces(0, 0, W.at[0]):
+            pltpu.make_async_copy(src, dst, w_sem.at[0]).start()
+
+    def wait_first():
+        mine = W.at[0, :, rows(me_s), :]
+        pltpu.make_async_copy(mine, mine, w_sem.at[0]).wait()
+        whole = W.at[0, :, rows(partner), :]
+        remote(whole, whole, ws_send.at[1, 0], w_recv.at[1, 2], to_partner).wait_recv()
+        for m in range(3):
+            pass_on(2, FIRST, partner, my, to_partner, m).wait_recv()
+            pass_on(4, FIRST, partner, 1 - my, to_partner, m).wait_recv()
+
+    def keep_first():
+        return pltpu.make_async_copy(W.at[0], wbuf.at[0, 0], keep_sem)
+
+    def free_first(_):
+        keep_first().wait()
+        for m in range(3):
+            for kind in (2, 3, 4):
+                pass_on(kind, FIRST, across, my, to_partner, m).wait_send()
 
     def wait_load(n):
         slot = lax.rem(n, 2)
@@ -196,7 +212,7 @@
     def c4_here(q, m):
         return pltpu.make_async_copy(piece.at[q, m], gfin.at[q, m, mine, :], out_sem.at[lax.rem(q, 2), m])
 
-    def g4(q, m):
+    def g4(q, m, then=None):
         slot = lax.rem(q, 2)
         for k in range(ZS - 1):
             c3(q, m, k).wait()
@@ -207,6 +223,8 @@
         piece[q, m] = v
         v = v.astype(f32)
         squares[...] += sum(v[:, i : i + LANES] * v[:, i : i + LANES] for i in range(0, F, LANES))
+        if then is not None:
+            then()
         for k in range(ZS - 1):
             c4(q, m, k).start()
         c4_here(q, m).start()
@@ -279,13 +297,16 @@
         g4(c, 1)
         each(g6)(b)
         g5(c, 0)
-        g4(c, 2)
-        over_r[me_r] = squares[...]
         peers_r = [to_peer(k) for k in range(YS * ZS - 1)]
         from_r = [lax.rem(me_r + YS * ZS - 1 - k, YS * ZS) for k in range(YS * ZS - 1)]
         peers_s = [{"r": me_r, "s": lax.rem(me_s + 1 + k, OWNERS)} for k in range(OWNERS - 1)]
         from_s = [lax.rem(me_s + OWNERS - 1 - k, OWNERS) for k in range(OWNERS - 1)]
-        tell(me_r, over_r, sn, rn, peers_r)
+
+        def tell_squares():
+            over_r[me_r] = squares[...]
+            tell(me_r, over_r, sn, rn, peers_r)
+
+        g4(c, 2, tell_squares)
         g5(c, 1)
         hear(me_r, over_r, sn, rn, peers_r, from_r)
         over_s[me_s] = jnp.sum(over_r[...], 0)
@@ -370,6 +391,7 @@
                 def _():
                     when(n + 1 < 2 * CHUNKS, forward2, n + 1)
                     when(n + 2 < 2 * CHUNKS, forward, n + 2)
+                    when(n == 1, free_first, n)
 
             when((b == 2) & (n + 1 < 3 * CHUNKS), load, n + 1)
             when((b == per - 1) & (n + 1 < 3 * CHUNKS), wait_load, n + 1)
@@ -393,6 +415,7 @@
     with jax.named_scope('barrier'):
         pl.semaphore_wait(barrier, len(peers))
     send_own(FIRST)
+    load_first()
     lax.fori_loop(1, 4, lambda c, _: (send_own(c), 0)[1], 0)
     load_x.wait()
 
@@ -412,9 +435,9 @@
             forward(FIRST, m)
         for m in range(3):
             forward2(FIRST, m)
-        load(FIRST)
         forward(1)
-        wait_load(0)
+        wait_first()
+        keep_first().start()
     with jax.named_scope('p_fwd'):
         phase(0, False, False)
     save_a.wait()
@@ -448,7 +471,14 @@
     with jax.named_scope('back'):
         lax.fori_loop(0, T // rb, back, 0)
         load_a.wait()
-    fetch = [pltpu.make_async_copy(src, dst, early_sem.at[i]) for i, (src, dst) in enumerate(zip(early, early_out))]
+    block = T // (4 * CHUNKS)
+    fetch = list(zip(early, early_out))
+    for i, w in enumerate((wg_hbm, wu_hbm)):
+        for l in range(2):
+            for k in range(CHUNKS):
+                there = H.at[pl.ds(((2 * i + l) * CHUNKS + k) * block, block), :]
+                fetch.append((w.at[l, :, pl.ds(k * F, F)], there))
+    fetch = [pltpu.make_async_copy(src, dst, early_sem.at[i]) for i, (src, dst) in enumerate(fetch)]
     for copy in fetch:
         copy.start()
     with jax.named_scope('p_zero'):
@@ -467,13 +497,11 @@
         one = wbuf.at[l, j, :, :HALF, :]
         remote(one, one, ws_send.at[0, q], w_recv.at[0, q + 2], to_across).wait_send()
 
-        def passed(each):
-            for m in each:
-                for kind in (2, 3, 4):
-                    pass_on(kind, q, across, my, to_partner, m).wait_send()
-
-        pl.when(q == 0)(lambda: passed(range(3)))
-        pl.when(q > 0)(lambda: passed([None]))
+        @pl.when(q > 0)
+        def _():
+            for kind in (2, 3, 4):
+                pass_on(kind, q, across, my, to_partner).wait_send()
+
         return 0
 
     for copy in fetch:
@@ -482,7 +510,7 @@
         lax.fori_loop(0, last, finish, 0)
 
 
-def gradients_of(x, dy, w_gate, w_up, w_down, early, tiles=(512, 256, 256), vmem=41 * 2**20):
+def gradients_of(x, dy, w_gate, w_up, w_down, early, tiles=(512, 256, 256), vmem=39 * 2**20):
     T, D = x.shape
     F = w_gate.shape[2] // CHUNKS
     Tt, rb, cb = tiles
@@ -495,21 +523,21 @@
     outs = pl.pallas_call(
         functools.partial(kernel, (T, D, F, Tt, rb, cb, lanes)),
         in_specs=[hbm] * (5 + len(early)),
-        out_specs=[hbm, pl.BlockSpec(memory_space=pltpu.VMEM), hbm, hbm] + [pl.BlockSpec(memory_space=pltpu.VMEM)] * len(early),
+        out_specs=[hbm, pl.BlockSpec(memory_space=pltpu.VMEM), hbm, hbm] + [pl.BlockSpec(memory_space=pltpu.VMEM)] * 6,
         out_shape=[
             pltpu.HBM((n, 3, R, F), bf16), pltpu.VMEM((8, 128), f32),
             pltpu.HBM((2, CHUNKS, 3, D, F), bf16), pltpu.HBM((T, D), bf16),
-            *(pltpu.VMEM(a.shape, a.dtype) for a in early),
+            *(pltpu.VMEM(a.shape, a.dtype) for a in early), pltpu.VMEM((T, D), bf16),
         ],
         scratch_shapes=[
-            vm((T, D), bf16), vm((T, D), bf16), vm((T, D), bf16), vm((T, D), f32),
+            vm((T, D), bf16), vm((T, D), bf16), vm((T, D), f32),
             vm((2, 3, D, F), bf16), vm((2, Tt, F), bf16), vm((2, Tt, F), bf16), vm((2, Tt, F), bf16), vm((3, D, F), f32),
             vm((3, XS, R, F), bf16), vm((2, 3, XS, R, F), bf16), vm((3, XS, R, F), f32),
             vm((3, R, F), bf16), vm((2, 3, R, F), bf16), vm((3, R, F), f32),
             vm((3, H, F), bf16), vm((2, 3, H, F), bf16), vm((3, H, F), f32),
             vm((3, ZS - 1, Q, F), bf16), vm((2, 3, ZS - 1, Q, F), bf16), vm((3, Q, F), f32),
             vm((n, 3, Q, F), bf16), vm((Q, lanes), f32), vm((YS * ZS, Q, lanes), f32), vm((OWNERS, Q, lanes), f32),
-            dma((2,)), dma((len(early),)), dma((2,)), dma((2, 3)),
+            dma((2,)), dma((5 + 4 * CHUNKS,)), dma((2,)), dma, dma((2, 3)),
             dma((2, n)), dma((3, n + 2)), dma((5, n + 2)),
             dma((3,)), dma((2, 3)), dma((3,)), dma((2, 3)), dma((3,)), dma((2, 3)), dma((3, ZS - 1)), dma((2, 3, ZS - 1)), dma((2, 3)), dma((2, 3)), dma((2, 3)), dma((2, 3)),
             dma((YS * ZS - 1,)), dma((YS * ZS - 1,)), dma((OWNERS - 1,)), dma((OWNERS - 1,)),
@@ -519,68 +547,57 @@
     return outs[0], outs[1], outs[4:]
 
 
-def update(factor, ga, gb, gc, *refs):
+def update(factor, ga, gb, gc, m_gate, m_up, m_down, v_gate, v_up, H, w_down, v_down, *outs):
     l, o = pl.program_id(0), pl.program_id(1)
     scale = factor[0:1, 0:1]
     for i, g in enumerate((ga, gb, gc)):
         _, parts, _, R, wide = g.shape
-        size = wide if i < 2 else R
         for j in range(parts):
-            near = slice(j * size, (j + 1) * size)
-            far = pl.ds(pl.multiple_of((o * parts + j) * size, size), size)
-
-            def read(kind):
-                ref, layer, cut = (refs[3 * kind + i], l, far) if (kind, i) in EARLY else (refs[3 * kind + i], 0, near)
-                return ref[layer, :, cut] if i < 2 else ref[layer, cut, :]
-
-            def write(kind, value):
-                if i < 2:
-                    refs[9 + 3 * kind + i][0, :, near] = value
-                else:
-                    refs[9 + 3 * kind + i][0, near, :] = value
-
+            if i < 2:
+                near = (slice(None), slice(j * wide, (j + 1) * wide))
+                far = (l, slice(None), pl.ds(pl.multiple_of((o * parts + j) * wide, wide), wide))
+                m, v = (m_gate, m_up)[i][far], (v_gate, v_up)[i][far]
+                row = ((2 * i + l) * CHUNKS + 2 * o + j // OWNERS) * R
+                w = H[pl.ds(pl.multiple_of(row, R), R), (j % OWNERS) * wide : (j % OWNERS + 1) * wide]
+            else:
+                near = (slice(j * R, (j + 1) * R), slice(None))
+                row = (o * parts + j) * R
+                w = w_down[0, *near]
+                m = m_down[l, pl.ds(pl.multiple_of(row, R), R), :]
+                v = v_down[0, *near]
             gradient = g[0, j, 0].astype(f32) * scale
-            m = 0.9 * read(1) + 0.1 * gradient
-            v = 0.95 * read(2) + 0.05 * gradient * gradient
-            w = read(0).astype(f32)
-            write(0, (w - 0.02 * (m * lax.rsqrt(v + 1e-8) + 0.1 * w)).astype(bf16))
-            write(1, m)
-            write(2, v)
-
-
-def updated(g, factor, weights, m, v):
+            w = w.astype(f32)
+            m = 0.9 * m + 0.1 * gradient
+            v = 0.95 * v + 0.05 * gradient * gradient
+            outs[i][0, *near] = (w - 0.02 * (m * lax.rsqrt(v + 1e-8) + 0.1 * w)).astype(bf16)
+            outs[3 + i][0, *near] = m
+            outs[6 + i][0, *near] = v
+
+
+def updated(g, factor, early, late, like):
     _, _, _, R, F = g.shape
     wide = F // OWNERS
     at = pl.BlockSpec
     native = [at((1, R, CHUNKS * wide), lambda l, o: (l, 0, o))] * 2 + [at((1, CHUNKS * R // OWNERS, F), lambda l, o: (l, o, 0))]
     mine = [at((1, CHUNKS, 1, R, wide), lambda l, o, k=k: (1 - l, 0, k, 0, o)) for k in range(2)]
     mine.append(at((1, CHUNKS // OWNERS, 1, R, F), lambda l, o: (1 - l, o, 2, 0, 0)))
-    arrays, specs = [], []
-    for kind, three in enumerate((weights, m, v)):
-        for i, a in enumerate(three):
-            early = (kind, i) in EARLY
-            arrays.append(pltpu.with_memory_space_constraint(a, pltpu.VMEM if early else pltpu.HBM))
-            specs.append(at(memory_space=pltpu.VMEM) if early else native[i])
     g = pltpu.with_memory_space_constraint(g, pltpu.HBM)
+    early = [pltpu.with_memory_space_constraint(a, pltpu.VMEM) for a in early]
     return pl.pallas_call(
         update,
         grid=(2, OWNERS),
-        in_specs=[at((8, 128), lambda l, o: (0, 0)), *mine, *specs],
+        in_specs=[at((8, 128), lambda l, o: (0, 0)), *mine, *[at(memory_space=pltpu.VMEM)] * len(early), native[2], native[2]],
         out_specs=native * 3,
-        out_shape=[jax.ShapeDtypeStruct(a.shape, a.dtype) for a in arrays],
-        compiler_params=pltpu.CompilerParams(vmem_limit_bytes=15 * 2**20),
-    )(factor, g, g, g, *arrays)
+        out_shape=[jax.ShapeDtypeStruct(a.shape, a.dtype) for a in like],
+        compiler_params=pltpu.CompilerParams(vmem_limit_bytes=14 * 2**20),
+    )(factor, g, g, g, *early, *(pltpu.with_memory_space_constraint(a, pltpu.HBM) for a in late))
 
 
 def solution(mesh, **options):
     def step(x, dy, *arrays):
         weights, m, v = (arrays[i : i + 3] for i in (0, 3, 6))
-        state = [weights, m, v]
-        g, factor, early = gradients_of(x[0], dy[0], *weights, [state[kind][i] for kind, i in EARLY], **options)
-        state = [list(three) for three in state]
-        for (kind, i), a in zip(EARLY, early):
-            state[kind][i] = a
-        return tuple(updated(g.reshape(2, CHUNKS, *g.shape[1:]), factor, *state))
+        g, factor, early = gradients_of(x[0], dy[0], *weights, [*m, *v[:2]], **options)
+        return tuple(updated(g.reshape(2, CHUNKS, *g.shape[1:]), factor, early, (weights[2], v[2]), arrays))
 
     states, cut = P(("rep", "r", "s"), None, None), P(None, "s", None)
     return jax.shard_map(

time: 431 us -> 428 us (level)
  no operation moved by 1% of the time
where the time goes in v4:
time: 428 us
  Pallas kernels  427 us (100%)
    pallas_call x1, Pallas kernels, gradients_of(): pl.pallas_call(functools.partial(kernel, (T, D, F, Tt, rb, cb, lanes)), i...  410 us
    pallas_call x1, Pallas kernels, updated(): pl.pallas_call(update, grid=(2, OWNERS), in_specs=[at((8, 128), lambda l,...  17.4 us

profile of v4, /device:TPU:0, one launch (start us, length us, event | category | flops | bytes accessed | tf_op | source)
XLA Modules:
  0.0 427.8 jit_solution(6085139918155985781)
XLA Ops:
  0.6 409.5 %shard_map.178 = (bf16[16,3,128,512]{3,2,1,0:T(8,128)(2,1)}, f32[8,128]{1,0:T(8,128)S(1)}, bf16[2,8,3,512,512]{4,3,2,1,0:T(8,128)(2,1)}, bf16[4096,512]{1,0:T(8,...) custom-call(bf16[4096,512]{1,0:T(8,128)(2,1)} %bitcast.6, ...), custom_call_target="tpu_custom_call" | custom-call | tf_op jit(solution)/shard_map/pallas_call | solution.py:523
  410.2 17.4 %shard_map.179 = (bf16[2,128,4096]{2,1,0:T(8,128)(2,1)}, bf16[2,128,4096]{2,1,0:T(8,128)(2,1)}, bf16[2,1024,512]{2,1,0:T(8,128)(2,1)}, f32[2,128,4096]{2,1,0:T(8...) custom-call(f32[8,128]{1,0:T(8,128)S(1)} %get-tuple-element.17.facto, ...), custom_call_target="tpu_custom_call" | custom-call | tf_op jit(solution)/shard_map/pallas_call | solution.py:586

commit v5 on v4

--- a/solution.py
+++ b/solution.py
@@ -367,17 +367,17 @@
 
     blocks = [(r, c) for r in range(Tt // rb) for c in range(F // cb)]
 
-    def together(w1, t1, slot1, w2, t2, slot2, backward, input_too, begin):
+    def together(w1, t1, slot1, w2, t2, slot2, backward, input_too, begin, ahead=True):
         for which in range(4 if input_too else 3) if backward else [0]:
             second(w2, t2, slot2, backward, input_too, begin, which)
-        for block in blocks:
+        for block in blocks if ahead else ():
             first(w1, t1, slot1, backward, *block)
 
     def phase(base, backward, input_too):
         for block in blocks:
             first(lax.rem(base, 2), 0, 0, backward, *block)
 
-        def step(i, _):
+        def step(final, i, _):
             n, b = base + i // per, lax.rem(i, per)
             if backward:
                 exchange(n - CHUNKS, b)
@@ -399,10 +399,11 @@
             t = 2 * b
             together(w, t + 1, 1, w, t, 0, backward, input_too, True)
             over = b == per - 1
-            together(jnp.where(over, 1 - w, w), jnp.where(over, 0, t + 2), 0, w, t + 1, 1, backward, input_too, False)
+            together(jnp.where(over, 1 - w, w), jnp.where(over, 0, t + 2), 0, w, t + 1, 1, backward, input_too, False, not final)
             return 0
 
-        lax.fori_loop(0, per * CHUNKS, step, 0)
+        lax.fori_loop(0, per * CHUNKS - 1, functools.partial(step, False), 0)
+        lax.fori_loop(per * CHUNKS - 1, per * CHUNKS, functools.partial(step, True), 0)
 
     barrier = pltpu.get_barrier_semaphore()
     peers = [to_partner, to_across] + [{"r": lax.rem(me_r + k, YS * ZS), "s": me_s} for k in range(1, YS * ZS)]

time: 428 us -> 426 us (level)
  no operation moved by 1% of the time
where the time goes in v5:
time: 426 us
  Pallas kernels  425 us (100%)
    pallas_call x1, Pallas kernels, gradients_of(): pl.pallas_call(functools.partial(kernel, (T, D, F, Tt, rb, cb, lanes)), i...  407 us
    pallas_call x1, Pallas kernels, updated(): pl.pallas_call(update, grid=(2, OWNERS), in_specs=[at((8, 128), lambda l,...  17.4 us

profile of v5, /device:TPU:0, one launch (start us, length us, event | category | flops | bytes accessed | tf_op | source)
XLA Modules:
  0.0 425.5 jit_solution(15474139332296383628)
XLA Ops:
  0.6 407.3 %shard_map.178 = (bf16[16,3,128,512]{3,2,1,0:T(8,128)(2,1)}, f32[8,128]{1,0:T(8,128)S(1)}, bf16[2,8,3,512,512]{4,3,2,1,0:T(8,128)(2,1)}, bf16[4096,512]{1,0:T(8,...) custom-call(bf16[4096,512]{1,0:T(8,128)(2,1)} %bitcast.6, ...), custom_call_target="tpu_custom_call" | custom-call | tf_op jit(solution)/shard_map/pallas_call | solution.py:524
  407.9 17.4 %shard_map.179 = (bf16[2,128,4096]{2,1,0:T(8,128)(2,1)}, bf16[2,128,4096]{2,1,0:T(8,128)(2,1)}, bf16[2,1024,512]{2,1,0:T(8,128)(2,1)}, f32[2,128,4096]{2,1,0:T(8...) custom-call(f32[8,128]{1,0:T(8,128)S(1)} %get-tuple-element.17.facto, ...), custom_call_target="tpu_custom_call" | custom-call | tf_op jit(solution)/shard_map/pallas_call | solution.py:587
